TPU v7x, 32 devices: a 4x4x1 block of a 4x4x8 slice. The times are simulated.
32 devices in a mesh: rep: 1 (over z), row: 4 (over y), col: 4 (over x), core: 2 (over core).
Axes of the slice: x: 4, y: 4, z: 1, core: 2. Of those that a mesh axis runs over, the one named last changes fastest.
The devices are a block of a 4x4x8 slice.
Arguments:
- x: bfloat16 [2, 512, 1280], P(None, ('rep', 'row', 'col', 'core'))
- route_idx: int32 [2, 512, 6], P(None, ('rep', 'row', 'col', 'core'))
- gates: float32 [2, 512, 6], P(None, ('rep', 'row', 'col', 'core'))
- w_gate: bfloat16 [160, 1280, 384], P(('rep', 'row', 'col', 'core'))
- w_up: bfloat16 [160, 1280, 384], P(('rep', 'row', 'col', 'core'))
- w_down: bfloat16 [160, 384, 1280], P(('rep', 'row', 'col', 'core'))
- grad_y: bfloat16 [2, 512, 1280], P(None, ('rep', 'row', 'col', 'core'))
Outputs:
- output 1: bfloat16 [2, 512, 1280], P(None, ('rep', 'row', 'col', 'core'))
- output 2: bfloat16 [2, 512, 1280], P(None, ('rep', 'row', 'col', 'core'))
- output 3: float32 [2, 512, 6], P(None, ('rep', 'row', 'col', 'core'))
- output 4: float32 [160, 1280, 384], P(('rep', 'row', 'col', 'core'))
- output 5: float32 [160, 1280, 384], P(('rep', 'row', 'col', 'core'))
- output 6: float32 [160, 384, 1280], P(('rep', 'row', 'col', 'core'))
All inputs are finite; a program needn't handle non-finite values.
Results may differ from a plain program's by a relative error of at most 0.00984795.
Values are sent between devices in bfloat16 or wider.
A program may use at most 768 MiB of HBM per device.

v0:
```python
import jax
import jax.numpy as jnp
from jax import lax
from jax.sharding import PartitionSpec as P

GROUP_AXES = ("row", "col", "core")
ALL_AXES = ("rep", "row", "col", "core")


def route_tables(route_ids, gates, group_size, capacity, local_experts):
    expert_ids = jnp.arange(group_size)[None, :] * local_experts + jnp.arange(local_experts)[:, None]
    expert_hits = route_ids[None, None, :, :] == expert_ids[:, :, None, None]
    member = jnp.sum(expert_hits.astype(jnp.int32), axis=3)
    slot_rank = jnp.cumsum(member, axis=2) - member
    disp_mask = (member[:, :, None, :] > 0) & (slot_rank[:, :, None, :] == jnp.arange(capacity)[None, None, :, None])
    slot_pos = jnp.sum(jnp.where(expert_hits, slot_rank[:, :, :, None], 0), axis=(0, 1))
    slot_addr = (route_ids % local_experts) * (group_size * capacity) + (route_ids // local_experts) * capacity + slot_pos
    row_gate = jnp.zeros((local_experts * group_size * capacity,), jnp.float32).at[slot_addr.reshape(-1)].set(gates.reshape(-1))
    return disp_mask.astype(jnp.bfloat16), slot_addr, row_gate


def expert_forward(x_rows, w_gate, w_up, w_down):
    gate_pre = jnp.einsum("lnd,ldf->lnf", x_rows, w_gate, preferred_element_type=jnp.float32).astype(jnp.bfloat16)
    up_pre = jnp.einsum("lnd,ldf->lnf", x_rows, w_up, preferred_element_type=jnp.float32).astype(jnp.bfloat16)
    gate_f = gate_pre.astype(jnp.float32)
    hidden = (gate_f * jax.nn.sigmoid(gate_f) * up_pre.astype(jnp.float32)).astype(jnp.bfloat16)
    exp_out = jnp.einsum("lnf,lfd->lnd", hidden, w_down, preferred_element_type=jnp.float32).astype(jnp.bfloat16)
    return exp_out, gate_pre, up_pre, hidden


def expert_backward(x_rows, d_out, gate_pre, up_pre, hidden, w_gate, w_up, w_down):
    gate_f = gate_pre.astype(jnp.float32)
    up_f = up_pre.astype(jnp.float32)
    sigmoid_g = jax.nn.sigmoid(gate_f)
    d_act = jnp.einsum("lnd,lfd->lnf", d_out, w_down, preferred_element_type=jnp.float32)
    d_up = (d_act * gate_f * sigmoid_g).astype(jnp.bfloat16)
    d_gate = (d_act * up_f * sigmoid_g * (1.0 + gate_f * (1.0 - sigmoid_g))).astype(jnp.bfloat16)
    g_down = jnp.einsum("lnf,lnd->lfd", hidden, d_out, preferred_element_type=jnp.float32)
    g_gate = jnp.einsum("lnd,lnf->ldf", x_rows, d_gate, preferred_element_type=jnp.float32)
    g_up = jnp.einsum("lnd,lnf->ldf", x_rows, d_up, preferred_element_type=jnp.float32)
    d_in = (jnp.einsum("lnf,ldf->lnd", d_gate, w_gate, preferred_element_type=jnp.float32) + jnp.einsum("lnf,ldf->lnd", d_up, w_up, preferred_element_type=jnp.float32)).astype(jnp.bfloat16)
    return d_in, g_gate, g_up, g_down


def solution(mesh):
    group_size = mesh.shape["row"] * mesh.shape["col"] * mesh.shape["core"]
    tok_spec = P(None, ALL_AXES, None)
    w_spec = P(ALL_AXES, None, None)

    def exchange(send_buf):
        return lax.all_to_all(send_buf, GROUP_AXES, 1, 1, tiled=True)

    def moe_layer(x, route_idx, gates, w_gate, w_up, w_down, grad_y):
        local_experts = w_gate.shape[0]
        tok_dev = x.shape[1]
        model_dim = x.shape[2]
        capacity = tok_dev // 2
        buf_rows = group_size * capacity
        buf_shape = (local_experts, group_size, capacity, model_dim)
        flat_shape = (local_experts * buf_rows, model_dim)
        outs_y, outs_dx, outs_dg = [], [], []
        sum_gate = jnp.zeros(w_gate.shape, jnp.float32)
        sum_up = jnp.zeros(w_up.shape, jnp.float32)
        sum_down = jnp.zeros(w_down.shape, jnp.float32)
        for micro_idx in range(2):
            x_mb = x[micro_idx]
            dy_mb = grad_y[micro_idx]
            gate_mb = gates[micro_idx]
            disp_mask, slot_addr, row_gate = route_tables(route_idx[micro_idx], gate_mb, group_size, capacity, local_experts)
            send_x = jnp.einsum("lgct,td->lgcd", disp_mask, x_mb, preferred_element_type=jnp.float32).astype(jnp.bfloat16)
            x_rows = exchange(send_x).reshape(local_experts, buf_rows, model_dim)
            exp_out, gate_pre, up_pre, hidden = expert_forward(x_rows, w_gate, w_up, w_down)
            out_back = exchange(exp_out.reshape(buf_shape)).reshape(flat_shape)
            out_slots = jnp.take(out_back, slot_addr, axis=0)
            outs_y.append(jnp.sum(gate_mb[:, :, None] * out_slots.astype(jnp.float32), axis=1).astype(jnp.bfloat16))
            outs_dg.append(jnp.einsum("td,tkd->tk", dy_mb, out_slots, preferred_element_type=jnp.float32))
            dy_rows = jnp.einsum("lgct,td->lgcd", disp_mask, dy_mb, preferred_element_type=jnp.float32)
            send_dout = (row_gate.reshape(local_experts, group_size, capacity)[..., None] * dy_rows).astype(jnp.bfloat16)
            d_out = exchange(send_dout).reshape(local_experts, buf_rows, model_dim)
            d_in, g_gate, g_up, g_down = expert_backward(x_rows, d_out, gate_pre, up_pre, hidden, w_gate, w_up, w_down)
            dx_back = exchange(d_in.reshape(buf_shape)).reshape(flat_shape)
            outs_dx.append(jnp.sum(jnp.take(dx_back, slot_addr, axis=0).astype(jnp.float32), axis=1).astype(jnp.bfloat16))
            sum_gate = sum_gate + g_gate
            sum_up = sum_up + g_up
            sum_down = sum_down + g_down
        return (jnp.stack(outs_y), jnp.stack(outs_dx), jnp.stack(outs_dg), sum_gate, sum_up, sum_down)

    return jax.shard_map(moe_layer, mesh=mesh, in_specs=(tok_spec, tok_spec, tok_spec, w_spec, w_spec, w_spec, tok_spec), out_specs=(tok_spec, tok_spec, tok_spec, w_spec, w_spec, w_spec), check_vma=False)
```

profile of v0, /device:TPU:98, one launch (start us, length us, event | category | flops | bytes accessed | tf_op | source)
XLA Modules:
  0.0 408.6 jit_solution(17749014959086169269)
XLA Ops:
  11.3 1.9 copy.171
  13.2 8.1 %all-to-all-start.6 = ((bf16[5,32,8,1280]{3,2,0,1:T(8,128)(2,1)}), bf16[5,32,8,1280]{3,2,0,1:T(8,128)(2,1)S(1)}, u32[]{:S(2)}, u32[]{:S(2)}) async-start(bf16[5,32,8,1280]{3,2,0,1:T(8,128)(2,1)} %copy.171), calls=%async_computation.6 | async-start | bytes 6553600 | tf_op jit(solution)/shard_map/all_to_all | solution.py:51
  23.1 1.9 copy.149
  25.0 39.9 %all-to-all-done.6 = bf16[5,32,8,1280]{3,2,0,1:T(8,128)(2,1)S(1)} async-done(((bf16[5,32,8,1280]{3,2,0,1:T(8,128)(2,1)}), bf16[5,32,8,1280]{3,2,0,1:T(8,128)(2,1)S(1)}, u32[]{:S(2)}, u32[]{:S(2)}) %all-to-all-start.6) | async-done | bytes 3276832 | tf_op jit(solution)/shard_map/all_to_all | solution.py:51
  66.5 3.1 all-to-all-start.2
  70.8 1.9 copy.136
  72.7 40.9 %all-to-all-done.2 = bf16[5,32,8,1280]{3,2,0,1:T(8,128)(2,1)S(1)} async-done(((bf16[5,32,8,1280]{3,2,0,1:T(8,128)(2,1)}), bf16[5,32,8,1280]{3,2,0,1:T(8,128)(2,1)S(1)}, u32[]{:S(2)}, u32[]{:S(2)}) %all-to-all-start.2) | async-done | bytes 3276832 | tf_op jit(solution)/shard_map/all_to_all | solution.py:51
  113.6 3.8 all-to-all-start
  121.7 1.9 copy.160
  123.6 37.7 %all-to-all-done = bf16[5,32,8,1280]{3,2,0,1:T(8,128)(2,1)} async-done(((bf16[5,32,8,1280]{3,2,0,1:T(8,128)(2,1)}), bf16[5,32,8,1280]{3,2,0,1:T(8,128)(2,1)}, u32[]{:S(2)}, u32[]{:S(2)}) %all-to-all-start) | async-done | bytes 3276832 | tf_op jit(solution)/shard_map/all_to_all | solution.py:51
  161.3 4.2 %all-to-all-start.4 = ((bf16[5,32,8,1280]{3,2,0,1:T(8,128)(2,1)}), bf16[5,32,8,1280]{3,2,0,1:T(8,128)(2,1)}, u32[]{:S(2)}, u32[]{:S(2)}) async-start(bf16[5,32,8,1280]{3,2,0,1:T(8,128)(2,1)} %copy.160), calls=%async_computation.4 | async-start | bytes 6553600 | tf_op jit(solution)/shard_map/all_to_all | solution.py:51
  165.5 5.4 %fusion.57 = bf16[5,256,384]{2,1,0:T(8,128)(2,1)S(1)} fusion(bf16[5,1280,384]{2,1,0:T(8,128)(2,1)} %param.12, bf16[5,32,8,1280]{3,2,0,1:T(8,128)(2,1)} %all-to-all-done), kind=kOutput, calls=%fused_computation.86 | convolution fusion | flops 1258782720 | bytes 9175040 | tf_op jit(solution)/shard_map/lnd,ldf->lnf/dot_general | solution.py:23
  170.9 5.6 %fusion.60 = bf16[5,256,384]{2,1,0:T(8,128)(2,1)S(1)} fusion(bf16[5,1280,384]{2,1,0:T(8,128)(2,1)} %param.13, bf16[5,32,8,1280]{3,2,0,1:T(8,128)(2,1)} %all-to-all-done), kind=kOutput, calls=%fused_computation.87 | convolution fusion | flops 1258782720 | bytes 9175040 | tf_op jit(solution)/shard_map/lnd,ldf->lnf/dot_general | solution.py:24
  176.6 1.9 fusion
  178.5 1.9 copy.138
  180.5 28.8 %all-to-all-done.4 = bf16[5,32,8,1280]{3,2,0,1:T(8,128)(2,1)} async-done(((bf16[5,32,8,1280]{3,2,0,1:T(8,128)(2,1)}), bf16[5,32,8,1280]{3,2,0,1:T(8,128)(2,1)}, u32[]{:S(2)}, u32[]{:S(2)}) %all-to-all-start.4) | async-done | bytes 3276832 | tf_op jit(solution)/shard_map/all_to_all | solution.py:51
  209.3 4.2 %all-to-all-start.1 = ((bf16[5,32,8,1280]{3,2,0,1:T(8,128)(2,1)}), bf16[5,32,8,1280]{3,2,0,1:T(8,128)(2,1)}, u32[]{:S(2)}, u32[]{:S(2)}) async-start(bf16[5,32,8,1280]{3,2,0,1:T(8,128)(2,1)} %copy.138), calls=%async_computation.1 | async-start | bytes 6553600 | tf_op jit(solution)/shard_map/all_to_all | solution.py:51
  214.8 4.4 %fusion.63 = bf16[5,256,384]{2,1,0:T(8,128)(2,1)S(1)} fusion(bf16[5,1280,384]{2,1,0:T(8,128)(2,1)} %param.12, bf16[5,32,8,1280]{3,2,0,1:T(8,128)(2,1)S(1)} %all-to-all-done.2), kind=kOutput, calls=%fused_computation.88 | convolution fusion | flops 1258782720 | bytes 9175040 | tf_op jit(solution)/shard_map/lnd,ldf->lnf/dot_general | solution.py:23
  219.3 4.6 %fusion.66 = bf16[5,256,384]{2,1,0:T(8,128)(2,1)S(1)} fusion(bf16[5,1280,384]{2,1,0:T(8,128)(2,1)} %param.13, bf16[5,32,8,1280]{3,2,0,1:T(8,128)(2,1)S(1)} %all-to-all-done.2), kind=kOutput, calls=%fused_computation.89 | convolution fusion | flops 1258782720 | bytes 9175040 | tf_op jit(solution)/shard_map/lnd,ldf->lnf/dot_general | solution.py:24
  223.9 1.9 fusion.1
  225.9 1.9 copy.151
  227.8 29.7 %all-to-all-done.1 = bf16[5,32,8,1280]{3,2,0,1:T(8,128)(2,1)} async-done(((bf16[5,32,8,1280]{3,2,0,1:T(8,128)(2,1)}), bf16[5,32,8,1280]{3,2,0,1:T(8,128)(2,1)}, u32[]{:S(2)}, u32[]{:S(2)}) %all-to-all-start.1) | async-done | bytes 3276832 | tf_op jit(solution)/shard_map/all_to_all | solution.py:51
  257.5 3.9 all-to-all-start.3
  261.5 5.9 %fusion.40 = (bf16[5,256,384]{2,1,0:T(8,128)(2,1)S(1)}, f32[5,256,384]{2,1,0:T(8,128)S(1)}) fusion(bf16[5,256,384]{2,1,0:T(8,128)(2,1)} %copy-done.38, bf16[5,256,384]{2,1,0:T(8,128)(2,1)} %copy-done.14, bf16[5,384,1280]{2,1,0:T(8,128)(2,1)} %param.14, bf16[5,32,8,1280]{3,2,0,1:T(8,128)(2,1)} %all-to-all-done.4), kind=kOutput, calls=%fused_computation.69 | convolution fusion | flops 1264189440 | bytes 13107200 | tf_op jit(solution)/shard_map/lnd,lfd->lnf/dot_general | solution.py:35
  267.4 5.4 %fusion.137 = f32[5,256,1280]{2,1,0:T(8,128)S(1)} fusion(bf16[5,256,384]{2,1,0:T(8,128)(2,1)S(1)} %get-tuple-element.51, bf16[5,1280,384]{2,1,0:T(8,128)(2,1)} %param.12), kind=kOutput, calls=%fused_computation.197 | convolution fusion | flops 1258291200 | bytes 12451840 | tf_op jit(solution)/shard_map/lnf,ldf->lnd/dot_general | solution.py:41
  272.9 4.4 %fusion.2 = bf16[5,32,8,1280]{3,2,1,0:T(8,128)(2,1)S(1)} fusion(f32[5,256,1280]{2,1,0:T(8,128)S(1)} %fusion.137, bf16[5,1280,384]{2,1,0:T(8,128)(2,1)} %param.13, f32[5,256,384]{2,1,0:T(8,128)S(1)} %get-tuple-element.52, bf16[5,256,384]{2,1,0:T(8,128)(2,1)S(1)} %copy-done.15), kind=kOutput, calls=%fused_computation.19 | convolution fusion | flops 1265008640 | bytes 17694720 | tf_op jit(solution)/shard_map/lnf,ldf->lnd/dot_general | solution.py:41
  277.3 1.9 copy.162
  280.9 6.0 %fusion.44 = (bf16[5,256,384]{2,1,0:T(8,128)(2,1)}, f32[5,256,384]{2,1,0:T(8,128)}) fusion(bf16[5,256,384]{2,1,0:T(8,128)(2,1)S(1)} %copy-done.20, bf16[5,256,384]{2,1,0:T(8,128)(2,1)S(1)} %copy-done.4, bf16[5,384,1280]{2,1,0:T(8,128)(2,1)} %param.14, bf16[5,32,8,1280]{3,2,0,1:T(8,128)(2,1)S(1)} %copy-done.1), kind=kOutput, calls=%fused_computation.73 | convolution fusion | flops 1264189440 | bytes 13107200 | tf_op jit(solution)/shard_map/lnd,lfd->lnf/dot_general | solution.py:35
  287.0 18.4 %all-to-all-done.3 = bf16[5,32,8,1280]{3,2,0,1:T(8,128)(2,1)} async-done(((bf16[5,32,8,1280]{3,2,0,1:T(8,128)(2,1)}), bf16[5,32,8,1280]{3,2,0,1:T(8,128)(2,1)}, u32[]{:S(2)}, u32[]{:S(2)}) %all-to-all-start.3) | async-done | bytes 3276832 | tf_op jit(solution)/shard_map/all_to_all | solution.py:51
  305.4 4.5 %all-to-all-start.5 = ((bf16[5,32,8,1280]{3,2,0,1:T(8,128)(2,1)}), bf16[5,32,8,1280]{3,2,0,1:T(8,128)(2,1)}, u32[]{:S(2)}, u32[]{:S(2)}) async-start(bf16[5,32,8,1280]{3,2,0,1:T(8,128)(2,1)} %copy.162), calls=%async_computation.5 | async-start | bytes 6553600 | tf_op jit(solution)/shard_map/all_to_all | solution.py:51
  309.8 4.7 %fusion.138 = f32[5,256,1280]{2,1,0:T(8,128)S(1)} fusion(bf16[5,256,384]{2,1,0:T(8,128)(2,1)} %get-tuple-element.49, bf16[5,1280,384]{2,1,0:T(8,128)(2,1)} %param.12), kind=kOutput, calls=%fused_computation.198 | convolution fusion | flops 1258291200 | bytes 12451840 | tf_op jit(solution)/shard_map/lnf,ldf->lnd/dot_general | solution.py:41
  314.6 4.4 %fusion.3 = bf16[5,32,8,1280]{3,2,1,0:T(8,128)(2,1)S(1)} fusion(f32[5,256,1280]{2,1,0:T(8,128)S(1)} %fusion.138, bf16[5,1280,384]{2,1,0:T(8,128)(2,1)} %param.13, f32[5,256,384]{2,1,0:T(8,128)S(1)} %copy-done.7, bf16[5,256,384]{2,1,0:T(8,128)(2,1)S(1)} %copy-done.5), kind=kOutput, calls=%fused_computation.20 | convolution fusion | flops 1265008640 | bytes 17694720 | tf_op jit(solution)/shard_map/lnf,ldf->lnd/dot_general | solution.py:41
  319.0 1.9 copy.173
  320.9 4.0 fusion.19
  325.0 7.9 %fusion.17 = f32[5,1280,384]{2,1,0:T(8,128)} fusion(bf16[5,32,8,1280]{3,2,0,1:T(8,128)(2,1)} %all-to-all-done, f32[5,256,384]{2,1,0:T(8,128)S(1)} %copy-done.10, bf16[5,256,384]{2,1,0:T(8,128)(2,1)S(1)} %copy-done.16), kind=kOutput, calls=%fused_computation.42 | convolution fusion | flops 1261731840 | bytes 16056320 | tf_op jit(solution)/shard_map/lnd,lnf->ldf/dot_general | solution.py:40
  332.8 5.8 %convolution_add_fusion.2 = f32[5,1280,384]{2,1,0:T(8,128)} fusion(f32[5,1280,384]{2,1,0:T(8,128)S(1)} %fusion.19, bf16[5,256,384]{2,1,0:T(8,128)(2,1)S(1)} %copy-done.13, bf16[5,32,8,1280]{3,2,0,1:T(8,128)(2,1)S(1)} %all-to-all-done.2), kind=kOutput, calls=%fused_computation.8 | convolution fusion | flops 1260748800 | bytes 23920640 | tf_op jit(solution)/shard_map/lnd,lnf->ldf/dot_general | solution.py:39
  338.7 15.0 %all-to-all-done.5 = bf16[5,32,8,1280]{3,2,0,1:T(8,128)(2,1)} async-done(((bf16[5,32,8,1280]{3,2,0,1:T(8,128)(2,1)}), bf16[5,32,8,1280]{3,2,0,1:T(8,128)(2,1)}, u32[]{:S(2)}, u32[]{:S(2)}) %all-to-all-start.5) | async-done | bytes 3276832 | tf_op jit(solution)/shard_map/all_to_all | solution.py:51
  353.6 4.8 %all-to-all-start.7 = ((bf16[5,32,8,1280]{3,2,0,1:T(8,128)(2,1)}), bf16[5,32,8,1280]{3,2,0,1:T(8,128)(2,1)}, u32[]{:S(2)}, u32[]{:S(2)}) async-start(bf16[5,32,8,1280]{3,2,0,1:T(8,128)(2,1)} %copy.173), calls=%async_computation.7 | async-start | bytes 6553600 | tf_op jit(solution)/shard_map/all_to_all | solution.py:51
  358.5 9.0 %fusion.7 = f32[5,384,1280]{2,1,0:T(8,128)} fusion(bf16[5,32,8,1280]{3,2,0,1:T(8,128)(2,1)} %all-to-all-done.4, bf16[5,256,384]{2,1,0:T(8,128)(2,1)} %copy-done.38, bf16[5,256,384]{2,1,0:T(8,128)(2,1)} %copy-done.14), kind=kOutput, calls=%fused_computation.32 | convolution fusion | flops 1262223360 | bytes 15073280 | tf_op jit(solution)/shard_map/lnf,lnd->lfd/dot_general | solution.py:38
  367.5 9.6 %convolution_add_fusion = f32[5,384,1280]{2,1,0:T(8,128)} fusion(f32[5,384,1280]{2,1,0:T(8,128)} %fusion.7, bf16[5,32,8,1280]{3,2,0,1:T(8,128)(2,1)S(1)} %copy-done.2, bf16[5,256,384]{2,1,0:T(8,128)(2,1)S(1)} %copy-done.21, bf16[5,256,384]{2,1,0:T(8,128)(2,1)S(1)} %copy-done.6), kind=kOutput, calls=%fused_computation.6 | convolution fusion | flops 1264680960 | bytes 24903680 | tf_op jit(solution)/shard_map/lnf,lnd->lfd/dot_general | solution.py:38
  377.1 6.0 %convolution_add_fusion.1 = f32[5,1280,384]{2,1,0:T(8,128)} fusion(f32[5,1280,384]{2,1,0:T(8,128)S(1)} %bitcast.133, bf16[5,32,8,1280]{3,2,0,1:T(8,128)(2,1)S(1)} %all-to-all-done.2, f32[5,256,384]{2,1,0:T(8,128)S(1)} %copy-done.8, bf16[5,256,384]{2,1,0:T(8,128)(2,1)S(1)} %copy-done.6), kind=kOutput, calls=%fused_computation.7 | convolution fusion | flops 1264189440 | bytes 25886720 | tf_op jit(solution)/shard_map/lnd,lnf->ldf/dot_general | solution.py:40
  383.1 2.1 copy.139
  387.5 2.2 copy.152
  392.5 2.1 copy.163
  396.4 2.0 multiply_reduce_fusion.1
  398.4 2.0 multiply_reduce_fusion
  400.3 1.9 all-to-all-done.7
  402.3 2.1 copy.174
  (175 shorter events, 33.1 us)
Async XLA Ops:
  8.3 4.9 %copy-start.30 = (s32[16,6]{0,1:T(8,128)}, s32[16,6]{0,1:T(8,128)S(1)}, u32[]{:S(2)}) copy-start(s32[16,6]{0,1:T(8,128)S(1)} %fusion.88) | copy-start | bytes 1156
  13.2 51.7 %all-to-all-start.6 = ((bf16[5,32,8,1280]{3,2,0,1:T(8,128)(2,1)}), bf16[5,32,8,1280]{3,2,0,1:T(8,128)(2,1)S(1)}, u32[]{:S(2)}, u32[]{:S(2)}) async-start(bf16[5,32,8,1280]{3,2,0,1:T(8,128)(2,1)} %copy.171), calls=%async_computation.6 | async-start | bytes 6553600 | tf_op jit(solution)/shard_map/all_to_all | solution.py:51
  25.0 44.8 %copy-start.23 = (bf16[2,16,1280]{2,1,0:T(8,128)(2,1)S(1)}, bf16[2,16,1280]{2,1,0:T(8,128)(2,1)}, u32[]{:S(2)}) copy-start(bf16[2,16,1280]{2,1,0:T(8,128)(2,1)} %param.9) | copy-start | bytes 245764
  66.5 47.1 %all-to-all-start.2 = ((bf16[5,32,8,1280]{3,2,0,1:T(8,128)(2,1)}), bf16[5,32,8,1280]{3,2,0,1:T(8,128)(2,1)S(1)}, u32[]{:S(2)}, u32[]{:S(2)}) async-start(bf16[5,32,8,1280]{3,2,0,1:T(8,128)(2,1)} %copy.149), calls=%async_computation.2 | async-start | bytes 6553600 | tf_op jit(solution)/shard_map/all_to_all | solution.py:51
  72.7 44.7 %copy-start.37 = (pred[1,16,6]{1,2,0:T(8,128)(4,1)S(1)}, pred[1,16,6]{1,2,0:T(8,128)(4,1)}, u32[]{:S(2)}) copy-start(pred[1,16,6]{1,2,0:T(8,128)(4,1)} %get-tuple-element.56) | copy-start | bytes 292
  72.7 44.9 %copy-start.36 = (f32[1,16,6]{1,0,2:T(1,128)S(1)}, f32[1,16,6]{1,0,2:T(1,128)}, u32[]{:S(2)}) copy-start(f32[1,16,6]{1,0,2:T(1,128)} %get-tuple-element.39) | copy-start | bytes 1156
  72.7 45.1 %copy-start.35 = (s32[1,16,6]{1,2,0:T(8,128)S(1)}, s32[1,16,6]{1,2,0:T(8,128)}, u32[]{:S(2)}) copy-start(s32[1,16,6]{1,2,0:T(8,128)} %get-tuple-element.54) | copy-start | bytes 1156
  72.7 45.3 %copy-start.34 = (s32[1,16,6]{1,2,0:T(8,128)S(1)}, s32[1,16,6]{1,2,0:T(8,128)}, u32[]{:S(2)}) copy-start(s32[1,16,6]{1,2,0:T(8,128)} %get-tuple-element.55) | copy-start | bytes 1156
  72.7 45.4 %copy-start.28 = (s32[16,6]{0,1:T(8,128)S(1)}, s32[16,6]{0,1:T(8,128)}, u32[]{:S(2)}) copy-start(s32[16,6]{0,1:T(8,128)} %get-tuple-element.31) | copy-start | bytes 1156
  72.7 47.9 %copy-start.22 = (bf16[2,16,1280]{2,1,0:T(8,128)(2,1)S(1)}, bf16[2,16,1280]{2,1,0:T(8,128)(2,1)}, u32[]{:S(2)}) copy-start(bf16[2,16,1280]{2,1,0:T(8,128)(2,1)} %param.15) | copy-start | bytes 245764
  113.6 47.6 %all-to-all-start = ((bf16[5,32,8,1280]{3,2,0,1:T(8,128)(2,1)}), bf16[5,32,8,1280]{3,2,0,1:T(8,128)(2,1)}, u32[]{:S(2)}, u32[]{:S(2)}) async-start(bf16[5,32,8,1280]{3,2,0,1:T(8,128)(2,1)} %copy.136), calls=%async_computation | async-start | bytes 6553600 | tf_op jit(solution)/shard_map/all_to_all | solution.py:51
  161.3 48.0 %all-to-all-start.4 = ((bf16[5,32,8,1280]{3,2,0,1:T(8,128)(2,1)}), bf16[5,32,8,1280]{3,2,0,1:T(8,128)(2,1)}, u32[]{:S(2)}, u32[]{:S(2)}) async-start(bf16[5,32,8,1280]{3,2,0,1:T(8,128)(2,1)} %copy.160), calls=%async_computation.4 | async-start | bytes 6553600 | tf_op jit(solution)/shard_map/all_to_all | solution.py:51
  165.5 11.1 %slice-start.3 = ((s8[4915200]{0:T(1024)(128)(4,1)}), s8[4194304]{0:T(1024)(128)(4,1)S(1)}, s32[]{:S(2)}) async-start(s8[4915200]{0:T(1024)(128)(4,1)} %bitcast.146), calls=%async_computation.11 | async-start | bytes 8388608
  170.9 5.6 %copy-start.14 = (bf16[5,256,384]{2,1,0:T(8,128)(2,1)}, bf16[5,256,384]{2,1,0:T(8,128)(2,1)S(1)}, u32[]{:S(2)}) copy-start(bf16[5,256,384]{2,1,0:T(8,128)(2,1)S(1)} %fusion.57) | copy-start | bytes 2949124
  170.9 5.7 %slice-start.4 = ((s8[4915200]{0:T(1024)(128)(4,1)}), s8[720896]{0:T(1024)(128)(4,1)S(1)}, s32[]{:S(2)}) async-start(s8[4915200]{0:T(1024)(128)(4,1)} %bitcast.146), calls=%async_computation.12 | async-start | bytes 1441792
  176.6 1.9 copy-start.38
  180.5 33.1 %copy-start.27 = (s32[1,16,6]{1,0,2:T(1,128)S(1)}, s32[1,16,6]{1,0,2:T(1,128)}, u32[]{:S(2)}) copy-start(s32[1,16,6]{1,0,2:T(1,128)} %copy-done.26) | copy-start | bytes 1156
  180.5 33.1 %copy-start.29 = (s32[16,6]{0,1:T(8,128)S(1)}, s32[16,6]{0,1:T(8,128)}, u32[]{:S(2)}) copy-start(s32[16,6]{0,1:T(8,128)} %get-tuple-element.31) | copy-start | bytes 1156
  180.5 33.4 %copy-start.31 = (s32[16,6]{0,1:T(8,128)S(1)}, s32[16,6]{0,1:T(8,128)}, u32[]{:S(2)}) copy-start(s32[16,6]{0,1:T(8,128)} %copy-done.30) | copy-start | bytes 1156
  209.3 48.2 %all-to-all-start.1 = ((bf16[5,32,8,1280]{3,2,0,1:T(8,128)(2,1)}), bf16[5,32,8,1280]{3,2,0,1:T(8,128)(2,1)}, u32[]{:S(2)}, u32[]{:S(2)}) async-start(bf16[5,32,8,1280]{3,2,0,1:T(8,128)(2,1)} %copy.138), calls=%async_computation.1 | async-start | bytes 6553600 | tf_op jit(solution)/shard_map/all_to_all | solution.py:51
  213.7 172.5 %copy-start.32 = (pred[16,6]{1,0:T(8,128)(4,1)}, pred[16,6]{1,0:T(8,128)(4,1)S(1)}, u32[]{:S(2)}) copy-start(pred[16,6]{1,0:T(8,128)(4,1)S(1)} %copy.134) | copy-start | bytes 292
  214.8 9.1 %slice-start.5 = ((s8[4915200]{0:T(1024)(128)(4,1)}), s8[4194304]{0:T(1024)(128)(4,1)S(1)}, s32[]{:S(2)}) async-start(s8[4915200]{0:T(1024)(128)(4,1)} %bitcast.148), calls=%async_computation.13 | async-start | bytes 8388608
  219.2 4.7 %copy-start.3 = (bf16[5,256,384]{2,1,0:T(8,128)(2,1)}, bf16[5,256,384]{2,1,0:T(8,128)(2,1)S(1)}, u32[]{:S(2)}) copy-start(bf16[5,256,384]{2,1,0:T(8,128)(2,1)S(1)} %fusion.63) | copy-start | bytes 2949124
  219.2 4.7 %slice-start.6 = ((s8[4915200]{0:T(1024)(128)(4,1)}), s8[720896]{0:T(1024)(128)(4,1)S(1)}, s32[]{:S(2)}) async-start(s8[4915200]{0:T(1024)(128)(4,1)} %bitcast.148), calls=%async_computation.14 | async-start | bytes 1441792
  223.9 1.9 copy-start.19
  257.5 47.8 %all-to-all-start.3 = ((bf16[5,32,8,1280]{3,2,0,1:T(8,128)(2,1)}), bf16[5,32,8,1280]{3,2,0,1:T(8,128)(2,1)}, u32[]{:S(2)}, u32[]{:S(2)}) async-start(bf16[5,32,8,1280]{3,2,0,1:T(8,128)(2,1)} %copy.151), calls=%async_computation.3 | async-start | bytes 6553600 | tf_op jit(solution)/shard_map/all_to_all | solution.py:51
  267.4 5.4 %copy-start.11 = (bf16[5,256,384]{2,1,0:T(8,128)(2,1)}, bf16[5,256,384]{2,1,0:T(8,128)(2,1)S(1)}, u32[]{:S(2)}) copy-start(bf16[5,256,384]{2,1,0:T(8,128)(2,1)S(1)} %get-tuple-element.51) | copy-start | bytes 2949124
  267.4 5.4 %copy-start.9 = (f32[5,256,384]{2,1,0:T(8,128)}, f32[5,256,384]{2,1,0:T(8,128)S(1)}, u32[]{:S(2)}) copy-start(f32[5,256,384]{2,1,0:T(8,128)S(1)} %get-tuple-element.52) | copy-start | bytes 5898244
  267.4 5.4 %copy-start.15 = (bf16[5,256,384]{2,1,0:T(8,128)(2,1)S(1)}, bf16[5,256,384]{2,1,0:T(8,128)(2,1)}, u32[]{:S(2)}) copy-start(bf16[5,256,384]{2,1,0:T(8,128)(2,1)} %copy-done.14) | copy-start | bytes 2949124
  277.3 3.1 copy-start.1
  277.3 3.4 copy-start.4
  277.3 3.6 copy-start.20
  305.4 48.3 %all-to-all-start.5 = ((bf16[5,32,8,1280]{3,2,0,1:T(8,128)(2,1)}), bf16[5,32,8,1280]{3,2,0,1:T(8,128)(2,1)}, u32[]{:S(2)}, u32[]{:S(2)}) async-start(bf16[5,32,8,1280]{3,2,0,1:T(8,128)(2,1)} %copy.162), calls=%async_computation.5 | async-start | bytes 6553600 | tf_op jit(solution)/shard_map/all_to_all | solution.py:51
  309.8 4.8 %copy-start.5 = (bf16[5,256,384]{2,1,0:T(8,128)(2,1)S(1)}, bf16[5,256,384]{2,1,0:T(8,128)(2,1)}, u32[]{:S(2)}) copy-start(bf16[5,256,384]{2,1,0:T(8,128)(2,1)} %copy-done.3) | copy-start | bytes 2949124
  309.8 4.8 %copy-start.7 = (f32[5,256,384]{2,1,0:T(8,128)S(1)}, f32[5,256,384]{2,1,0:T(8,128)}, u32[]{:S(2)}) copy-start(f32[5,256,384]{2,1,0:T(8,128)} %get-tuple-element.50) | copy-start | bytes 5898244
  319.0 1.9 copy-start.12
  320.9 4.0 copy-start.10
  320.9 4.0 copy-start.16
  325.0 7.9 %copy-start.13 = (bf16[5,256,384]{2,1,0:T(8,128)(2,1)S(1)}, bf16[5,256,384]{2,1,0:T(8,128)(2,1)}, u32[]{:S(2)}) copy-start(bf16[5,256,384]{2,1,0:T(8,128)(2,1)} %get-tuple-element.49) | copy-start | bytes 2949124
  353.6 48.6 %all-to-all-start.7 = ((bf16[5,32,8,1280]{3,2,0,1:T(8,128)(2,1)}), bf16[5,32,8,1280]{3,2,0,1:T(8,128)(2,1)}, u32[]{:S(2)}, u32[]{:S(2)}) async-start(bf16[5,32,8,1280]{3,2,0,1:T(8,128)(2,1)} %copy.173), calls=%async_computation.7 | async-start | bytes 6553600 | tf_op jit(solution)/shard_map/all_to_all | solution.py:51
  358.4 9.0 %copy-start.2 = (bf16[5,32,8,1280]{3,2,0,1:T(8,128)(2,1)S(1)}, bf16[5,32,8,1280]{3,2,0,1:T(8,128)(2,1)}, u32[]{:S(2)}) copy-start(bf16[5,32,8,1280]{3,2,0,1:T(8,128)(2,1)} %copy-done) | copy-start | bytes 9830404
  358.5 9.0 %copy-start.6 = (bf16[5,256,384]{2,1,0:T(8,128)(2,1)S(1)}, bf16[5,256,384]{2,1,0:T(8,128)(2,1)}, u32[]{:S(2)}) copy-start(bf16[5,256,384]{2,1,0:T(8,128)(2,1)} %copy-done.3) | copy-start | bytes 2949124
  358.5 9.0 %copy-start.21 = (bf16[5,256,384]{2,1,0:T(8,128)(2,1)S(1)}, bf16[5,256,384]{2,1,0:T(8,128)(2,1)}, u32[]{:S(2)}) copy-start(bf16[5,256,384]{2,1,0:T(8,128)(2,1)} %copy-done.19) | copy-start | bytes 2949124
  358.5 18.6 %slice-start = ((s8[9830400]{0:T(1024)(128)(4,1)}), s8[4194304]{0:T(1024)(128)(4,1)S(1)}, s32[]{:S(2)}) async-start(s8[9830400]{0:T(1024)(128)(4,1)} %bitcast.132), calls=%async_computation.8 | async-start | bytes 8388608
  358.5 18.6 %slice-start.1 = ((s8[9830400]{0:T(1024)(128)(4,1)}), s8[4194304]{0:T(1024)(128)(4,1)S(1)}, s32[]{:S(2)}) async-start(s8[9830400]{0:T(1024)(128)(4,1)} %bitcast.132), calls=%async_computation.9 | async-start | bytes 8388608
  367.5 9.6 %slice-start.2 = ((s8[9830400]{0:T(1024)(128)(4,1)}), s8[1441792]{0:T(1024)(128)(4,1)S(1)}, s32[]{:S(2)}) async-start(s8[9830400]{0:T(1024)(128)(4,1)} %bitcast.132), calls=%async_computation.10 | async-start | bytes 2883584
  367.5 9.6 %copy-start.8 = (f32[5,256,384]{2,1,0:T(8,128)S(1)}, f32[5,256,384]{2,1,0:T(8,128)}, u32[]{:S(2)}) copy-start(f32[5,256,384]{2,1,0:T(8,128)} %get-tuple-element.50) | copy-start | bytes 5898244
  394.6 1.8 copy-start.25
  (6 other events, 7.1 us)
where the time goes:
time: 416 us; the launch traced here: 409 us
  waiting for transfers between devices  212 us (51%)
  matrix products  105 us (25%)
  local copies, waits for them, and re-layouts  40.7 us (10%)
  starting transfers between devices  36.6 us (9%)
  other arithmetic  12.2 us (3%)
    all_to_all x8, waiting for transfers between devices, exchange(): return lax.all_to_all(send_buf, GROUP_AXES, 1, 1, tiled=True)  212 us
    all_to_all x8, starting transfers between devices, exchange(): return lax.all_to_all(send_buf, GROUP_AXES, 1, 1, tiled=True)  36.6 us
    dot_general x2, matrix products, expert_backward(): jnp.einsum('lnf,lnd->lfd', hidden, d_out, preferred_element_type=jnp.floa...  18.6 us
    dot_general x2, matrix products, expert_backward(): jnp.einsum('lnd,lnf->ldf', x_rows, d_up, preferred_element_type=jnp.float32)  13.8 us
    dot_general x2, matrix products, expert_backward(): jnp.einsum('lnd,lfd->lnf', d_out, w_down, preferred_element_type=jnp.floa...  12 us
    dot_general x2, matrix products, expert_forward(): jnp.einsum('lnd,ldf->lnf', x_rows, w_up, preferred_element_type=jnp.float32)  10.2 us
    dot_general x2, matrix products, expert_backward(): jnp.einsum('lnf,ldf->lnd', d_gate, w_gate, preferred_element_type=jnp.flo...  10.1 us
    dot_general x2, matrix products, expert_backward(): jnp.einsum('lnd,lnf->ldf', x_rows, d_gate, preferred_element_type=jnp.flo...  9.81 us
  transfers between devices with their start and end apart: 8, of which 8 were waited for; matrix products, arithmetic and copies ran while one was open for 33% of the time, Pallas kernels for 0%

commit v1 on v0

v1 whole, which is shorter than its diff:
```python
import functools

import jax
import jax.numpy as jnp
from jax import lax
from jax.experimental import pallas as pl
from jax.experimental.pallas import tpu as pltpu
from jax.sharding import PartitionSpec as P

GROUP_AXES = ("row", "col", "core")
ALL_AXES = ("rep", "row", "col", "core")
F32 = jnp.float32
BF16 = jnp.bfloat16
LANES = 128
SMALL = 32


def dot_nn(a, b):
    return lax.dot_general(a, b, (((1,), (0,)), ((), ())), preferred_element_type=F32)


def dot_nt(a, b):
    return lax.dot_general(a, b, (((1,), (1,)), ((), ())), preferred_element_type=F32)


def dot_tn(a, b):
    return lax.dot_general(a, b, (((0,), (0,)), ((), ())), preferred_element_type=F32)


def split3(v):
    h1 = v.astype(BF16)
    r1 = v - h1.astype(F32)
    h2 = r1.astype(BF16)
    h3 = (r1 - h2.astype(F32)).astype(BF16)
    return h1, h2, h3


def col_blocks(width, step):
    return [(s, min(step, width - s)) for s in range(0, width, step)]


def expert_kernel(dims, xd_hbm, wg_hbm, wu_hbm, wd_hbm, part_hbm, gg_hbm, gu_hbm, gd_hbm,
                  xd_v, pt_v, gr_v, acc_v, wg_v, wu_v, wd_v, og_v, ou_v, od_v, pos_v,
                  xt_v, qt_v, a_v, duv_v, cnt_s, base_s, sem_x, sem_w, sem_o, sem_p):
    tokens, dm, ff, el, top_k, seg = dims
    n_row, n_col, n_core = lax.axis_size("row"), lax.axis_size("col"), lax.axis_size("core")
    me = (lax.axis_index("row") * n_col + lax.axis_index("col")) * n_core + lax.axis_index("core")
    width = 2 * dm + LANES

    def load_w(e, slot):
        return [pltpu.make_async_copy(h.at[e], v.at[slot], sem_w.at[slot, i])
                for i, (h, v) in enumerate(((wg_hbm, wg_v), (wu_hbm, wu_v), (wd_hbm, wd_v)))]

    def store_g(e, slot):
        return [pltpu.make_async_copy(v.at[slot], h.at[e], sem_o.at[slot, i])
                for i, (h, v) in enumerate(((gg_hbm, og_v), (gu_hbm, ou_v), (gd_hbm, od_v)))]

    loads_x = [pltpu.make_async_copy(xd_hbm.at[m], xd_v.at[m], sem_x.at[m]) for m in range(2)]
    for c in loads_x:
        c.start()
    for s in range(2):
        for c in load_w(s, s):
            c.start()

    row_i = lax.broadcasted_iota(jnp.int32, (tokens, tokens), 0)
    col_i = lax.broadcasted_iota(jnp.int32, (tokens, tokens), 1)
    tri = (row_i < col_i).astype(F32).astype(BF16)
    sub = lax.broadcasted_iota(jnp.int32, (8, tokens), 0)
    eids = jnp.where(sub < el, (me * el + sub), -1).astype(F32)

    def chunks(total):
        return jnp.maximum((total + (seg - 1)) // seg, 1)

    n_chunks = []
    for m in range(2):
        loads_x[m].wait()
        meta_t = xd_v[m, :, 2 * dm:].astype(F32).T
        hits = jnp.zeros((8, tokens), F32)
        for j in range(top_k):
            hits = hits + (meta_t[j:j + 1, :] == eids).astype(F32)
        rank = dot_nn(hits.astype(BF16), tri)
        total = jnp.int32(0)
        for e in range(el):
            cnt = jnp.sum(hits[e:e + 1, :]).astype(jnp.int32)
            cnt_s[m, e] = cnt
            base_s[m, e] = total
            pos_v[m, e:e + 1, :] = jnp.where(hits[e:e + 1, :] > 0, rank[e:e + 1, :] + total.astype(F32), -1.0)
            total = total + (cnt + 15) // 16 * 16
        n_ch = chunks(total)
        n_chunks.append(n_ch)

        def gather(c, carry, m=m):
            off = pl.multiple_of(c * seg, seg)
            rows = (lax.broadcasted_iota(jnp.int32, (seg, tokens), 0) + off).astype(F32)
            pick = rows == pos_v[m, 0:1, :]
            for e in range(1, el):
                pick = pick | (rows == pos_v[m, e:e + 1, :])
            pick_f = pick.astype(F32)
            pt_v[m, :, pl.ds(off, seg)] = pick_f.T.astype(BF16)
            pick_b = pick_f.astype(BF16)
            for s, w in col_blocks(width, 512):
                gr_v[m, pl.ds(off, seg), s:s + w] = dot_nn(pick_b, xd_v[m, :, s:s + w]).astype(BF16)
            return carry

        lax.fori_loop(0, n_ch, gather, 0)

    def tile(e, slot, ra, rb, m_a, n_a, n_b, first):
        rows = ra + rb
        base_a = pl.multiple_of(base_s[m_a, e], 16)
        base_b = pl.multiple_of(base_s[1 - m_a, e], 16)
        it = lax.broadcasted_iota(jnp.int32, (rows, 1), 0)
        valid = ((it < ra) & (it < n_a)) | ((it >= ra) & (it - ra < n_b))

        def read(s, w):
            return jnp.concatenate([gr_v[m_a, pl.ds(base_a, ra), s:s + w],
                                    gr_v[1 - m_a, pl.ds(base_b, rb), s:s + w]], axis=0)

        def write(s, w, val):
            merged = jnp.where(valid, val.astype(F32), read(s, w).astype(F32)).astype(BF16)
            gr_v[m_a, pl.ds(base_a, ra), s:s + w] = merged[:ra]

            @pl.when(n_b > 0)
            def _():
                gr_v[1 - m_a, pl.ds(base_b, rb), s:s + w] = merged[ra:]

        lane = lax.broadcasted_iota(jnp.int32, (rows, LANES), 1)
        meta = jnp.where(valid, read(2 * dm, LANES).astype(F32), 0.0)
        eid = (me * el + e).astype(F32)
        mine = ((meta == eid) & (lane < top_k)).astype(F32)
        sel = pltpu.roll(mine, 8, 1) + pltpu.roll(mine, 16, 1) + pltpu.roll(mine, 24, 1)
        gate = jnp.where(valid, jnp.sum(meta * sel, axis=1, keepdims=True), 0.0)
        for s, w in col_blocks(dm, 256):
            xt_v[:rows, s:s + w] = jnp.where(valid, read(s, w).astype(F32), 0.0).astype(BF16)
            dy = jnp.where(valid, read(dm + s, w).astype(F32), 0.0)
            qt_v[:rows, s:s + w] = (gate * dy).astype(BF16)
        xt = xt_v[:rows, :]
        u = dot_nn(xt, wg_v[slot]).astype(BF16).astype(F32)
        v = dot_nn(xt, wu_v[slot]).astype(BF16).astype(F32)
        r = dot_nt(qt_v[:rows, :], wd_v[slot])
        s_g = jax.nn.sigmoid(u)
        a_v[:rows, :] = (u * s_g * v).astype(BF16)
        duv_v[:rows, :ff] = (r * v * s_g * (1.0 + u * (1.0 - s_g))).astype(BF16)
        duv_v[:rows, ff:] = (r * u * s_g).astype(BF16)
        a = a_v[:rows, :]
        du = duv_v[:rows, :ff]
        dv = duv_v[:rows, ff:]
        dots = jnp.zeros((rows, 1), F32)
        for s, w in col_blocks(dm, 256):
            o = dot_nn(a, wd_v[slot, :, s:s + w]).astype(BF16)
            dy = jnp.where(valid, read(dm + s, w).astype(F32), 0.0)
            dots = dots + jnp.sum(dy * o.astype(F32), axis=1, keepdims=True)
            write(s, w, o)
        for s, w in col_blocks(dm, 256):
            p = dot_nt(du, wg_v[slot, s:s + w, :]) + dot_nt(dv, wu_v[slot, s:s + w, :])
            write(dm + s, w, p.astype(BF16))
        d1, d2, d3 = split3(dots)
        g1, g2, g3 = split3(gate)
        new_meta = jnp.zeros((rows, LANES), F32)
        for at, val in ((e, d1), (8 + e, d2), (16 + e, d3), (32, g1), (33, g2), (34, g3)):
            new_meta = jnp.where(lane == at, val.astype(F32), new_meta)
        write(2 * dm, LANES, new_meta)

        def put(ref, idx, val):
            if first is None:
                ref[idx] = val
            else:
                ref[idx] = jnp.where(first, 0.0, ref[idx]) + val

        duv = duv_v[:rows, :]
        for s, w in col_blocks(dm, 256):
            g_in = dot_tn(xt_v[:rows, s:s + w], duv)
            put(og_v, (slot, slice(s, s + w)), g_in[:, :ff])
            put(ou_v, (slot, slice(s, s + w)), g_in[:, ff:])
        for s, w in col_blocks(dm, 256):
            put(od_v, (slot, slice(None), slice(s, s + w)), dot_tn(a, qt_v[:rows, s:s + w]))

    def expert(e, carry):
        slot = lax.rem(e, 2)
        for c in load_w(e, slot):
            c.wait()

        @pl.when(e >= 2)
        def _():
            for c in store_g(e - 2, slot):
                c.wait()

        n0, n1 = cnt_s[0, e], cnt_s[1, e]
        big0, big1 = n0 > SMALL, n1 > SMALL

        @pl.when(jnp.logical_not(big0 | big1))
        def _():
            tile(e, slot, SMALL, SMALL, 0, n0, n1, None)

        @pl.when(big0 | big1)
        def _():
            both = big0 & big1

            def one(i, inner):
                m_a = jnp.where(both, i, jnp.where(big0, 0, 1))
                n_a = jnp.where(m_a == 0, n0, n1)
                n_b = jnp.where(both, 0, jnp.where(m_a == 0, n1, n0))
                tile(e, slot, seg, SMALL, m_a, n_a, n_b, i == 0)
                return inner

            lax.fori_loop(0, jnp.where(both, 2, 1), one, 0)

        for c in store_g(e, slot):
            c.start()

        @pl.when(e + 2 < el)
        def _():
            for c in load_w(e + 2, slot):
                c.start()

        return carry

    lax.fori_loop(0, el, expert, 0)

    for m in range(2):
        def scatter(c, carry, m=m):
            off = pl.multiple_of(c * seg, seg)
            rows = pl.ds(off, seg)
            first = c == 0
            pt = pt_v[m, :, rows]
            gp = gr_v[m, rows, 2 * dm:].astype(F32)
            gate = gp[:, 32:33] + gp[:, 33:34] + gp[:, 34:35]
            for s, w in col_blocks(dm, 256):
                h1, h2, h3 = split3(gate * gr_v[m, rows, s:s + w].astype(F32))
                add = dot_nn(pt, h1) + dot_nn(pt, h2) + dot_nn(pt, h3)
                acc_v[m, :, s:s + w] = jnp.where(first, 0.0, acc_v[m, :, s:s + w]) + add
            for s, w in col_blocks(dm + LANES, 256):
                lo = dm + s
                add = dot_nn(pt, gr_v[m, rows, lo:lo + w])
                acc_v[m, :, lo:lo + w] = jnp.where(first, 0.0, acc_v[m, :, lo:lo + w]) + add
            return carry

        lax.fori_loop(0, n_chunks[m], scatter, 0)
        lane = lax.broadcasted_iota(jnp.int32, (tokens, LANES), 1)
        ids = jnp.where(lane < top_k, xd_v[m, :, 2 * dm:].astype(F32), -1.0)
        raw = acc_v[m, :, 2 * dm:]
        out = jnp.zeros((tokens, LANES), F32)
        for e in range(el):
            val = raw[:, e:e + 1] + raw[:, 8 + e:9 + e] + raw[:, 16 + e:17 + e]
            out = jnp.where(ids == (me * el + e).astype(F32), val, out)
        acc_v[m, :, 2 * dm:] = out
        pltpu.make_async_copy(acc_v.at[m], part_hbm.at[m], sem_p.at[m]).start()

    for e in range(el - 2, el):
        for c in store_g(e, e % 2):
            c.wait()
    for m in range(2):
        pltpu.make_async_copy(acc_v.at[m], part_hbm.at[m], sem_p.at[m]).wait()


def expert_stage(xd, w_gate, w_up, w_down, top_k, seg):
    _, tokens, width = xd.shape
    el, dm, ff = w_gate.shape
    any_spec = pl.BlockSpec(memory_space=pl.ANY)
    rows_max = el * seg
    tile_rows = seg + SMALL
    dims = (tokens, dm, ff, el, top_k, seg)
    return pl.pallas_call(
        functools.partial(expert_kernel, dims),
        out_shape=(
            jax.ShapeDtypeStruct((2, tokens, width), F32),
            jax.ShapeDtypeStruct((el, dm, ff), F32),
            jax.ShapeDtypeStruct((el, dm, ff), F32),
            jax.ShapeDtypeStruct((el, ff, dm), F32),
        ),
        in_specs=[any_spec] * 4,
        out_specs=[any_spec] * 4,
        scratch_shapes=[
            pltpu.VMEM((2, tokens, width), BF16),
            pltpu.VMEM((2, tokens, rows_max), BF16),
            pltpu.VMEM((2, rows_max, width), BF16),
            pltpu.VMEM((2, tokens, width), F32),
            pltpu.VMEM((2, dm, ff), BF16),
            pltpu.VMEM((2, dm, ff), BF16),
            pltpu.VMEM((2, ff, dm), BF16),
            pltpu.VMEM((2, dm, ff), F32),
            pltpu.VMEM((2, dm, ff), F32),
            pltpu.VMEM((2, ff, dm), F32),
            pltpu.VMEM((2, 8, tokens), F32),
            pltpu.VMEM((tile_rows, dm), BF16),
            pltpu.VMEM((tile_rows, dm), BF16),
            pltpu.VMEM((tile_rows, ff), BF16),
            pltpu.VMEM((tile_rows, 2 * ff), BF16),
            pltpu.SMEM((2, 8), jnp.int32),
            pltpu.SMEM((2, 8), jnp.int32),
            pltpu.SemaphoreType.DMA((2,)),
            pltpu.SemaphoreType.DMA((2, 3)),
            pltpu.SemaphoreType.DMA((2, 3)),
            pltpu.SemaphoreType.DMA((2,)),
        ],
        compiler_params=pltpu.CompilerParams(vmem_limit_bytes=66_000_000),
        name="experts",
    )(xd, w_gate, w_up, w_down)


def pack_tokens(x, route_idx, gates, grad_y):
    def piece(v):
        return lax.reduce_precision(v, 8, 7)

    g1 = piece(gates)
    g2 = piece(gates - g1)
    g3 = piece(gates - g1 - g2)

    def pad(v):
        return jnp.pad(v.astype(BF16), ((0, 0), (0, 0), (0, 8 - v.shape[2])))

    ids = route_idx.astype(F32)
    meta = jnp.concatenate([pad(ids), pad(g1), pad(g2), pad(g3)], axis=2)
    meta = jnp.pad(meta, ((0, 0), (0, 0), (0, LANES - meta.shape[2])))
    return jnp.concatenate([x, grad_y, meta], axis=2)


def solution(mesh):
    group = mesh.shape["row"] * mesh.shape["col"] * mesh.shape["core"]
    tok_spec = P(None, ALL_AXES, None)
    w_spec = P(ALL_AXES, None, None)

    def moe_layer(x, route_idx, gates, w_gate, w_up, w_down, grad_y):
        _, tok_dev, dm = x.shape
        top_k = route_idx.shape[2]
        packed = pack_tokens(x, route_idx, gates, grad_y)
        xd = lax.all_gather(packed, GROUP_AXES, axis=1, tiled=True)
        part, g_gate, g_up, g_down = expert_stage(xd, w_gate, w_up, w_down, top_k, group * (tok_dev // 2))
        mine = lax.psum_scatter(part, GROUP_AXES, scatter_dimension=1, tiled=True)
        y = mine[:, :, :dm].astype(BF16)
        dx = mine[:, :, dm:2 * dm].astype(BF16)
        dg = mine[:, :, 2 * dm:2 * dm + top_k]
        return y, dx, dg, g_gate, g_up, g_down

    return jax.shard_map(moe_layer, mesh=mesh, in_specs=(tok_spec, tok_spec, tok_spec, w_spec, w_spec, w_spec, tok_spec), out_specs=(tok_spec, tok_spec, tok_spec, w_spec, w_spec, w_spec), check_vma=False)
```

time: 416 us -> 205 us (0.49)
  the two profiles are of different devices: /device:TPU:98 before, /device:TPU:97 now
where the time goes in v1:
time: 205 us; the launch traced here: 204 us
  waiting for transfers between devices  147 us (72%)
  Pallas kernels  36.1 us (18%)
  between operations  14.1 us (7%)
  local copies, waits for them, and re-layouts  3.62 us (2%)
  other arithmetic  2.71 us (1%)
    reduce_scatter x1, waiting for transfers between devices, moe_layer(): mine = lax.psum_scatter(part, GROUP_AXES, scatter_dimension=1, tiled=True)  100 us
    all_gather x1, waiting for transfers between devices, moe_layer(): xd = lax.all_gather(packed, GROUP_AXES, axis=1, tiled=True)  47 us
    pallas_call x1, Pallas kernels, expert_stage(): pl.pallas_call(functools.partial(expert_kernel, dims), out_shape=(jax.Sha...  36.1 us
  transfers between devices with their start and end apart: 2, of which 2 were waited for; matrix products, arithmetic and copies ran while one was open for 0% of the time, Pallas kernels for 0%

profile of v1, /device:TPU:97, one launch (start us, length us, event | category | flops | bytes accessed | tf_op | source)
XLA Modules:
  0.0 204.1 jit_solution(7666350963793084874)
XLA Ops:
  7.2 0.1 all-gather.2.cloned.1.call-start
  7.2 0.8 copy.13
  8.0 0.8 copy.14
  8.8 0.1 fusion.11
  8.9 1.6 fusion.1
  10.5 0.1 all-gather.2.cloned.1.call-update
  10.6 0.1 reduce-scatter.2.cloned.1.call-start
  10.6 47.0 %all-gather.2.cloned.1.call-done.xd_hbm = bf16[2,512,2688]{2,1,0:T(8,128)(2,1)} async-done(((bf16[2,16,2688]{2,1,0:T(8,128)(2,1)}), bf16[2,512,2688]{2,1,0:T(8,128)(2,1)}) %all-gather.2.cloned.1.call-update) | async-done | bytes 5505040 | tf_op jit(solution)/shard_map/all_gather | solution.py:326
  57.6 36.1 %experts.1 = (f32[2,512,2688]{2,1,0:T(8,128)}, f32[5,1280,384]{2,1,0:T(8,128)}, f32[5,1280,384]{2,1,0:T(8,128)}, f32[5,384,1280]{2,1,0:T(8,128)}) custom-call(bf16[2,512,2688]{2,1,0:T(8,128)(2,1)} %all-gather.2.cloned.1.call-done.xd_hbm, bf16[5,1280,384]{2,1,0:T(8,128)(2,1)} %wg_hbm.1, bf16[5,1280,384]{2,1,0:T(8,128)(2,1)} %wu_hbm.1, ...), custom_call_target="tpu_custom_call" | custom-call | tf_op jit(solution)/shard_map/experts/pallas_call | solution.py:262
  93.7 0.1 reduce-scatter.2.cloned.1.call-update
  93.8 100.4 %reduce-scatter.2.cloned.1.call-done = f32[2,16,2688]{2,1,0:T(8,128)} async-done(((f32[2,512,2688]{2,1,0:T(8,128)}), f32[2,16,2688]{2,1,0:T(8,128)}) %reduce-scatter.2.cloned.1.call-update) | async-done | bytes 344080 | tf_op jit(solution)/shard_map/reduce_scatter | solution.py:328
  194.2 0.7 slice.16
  194.9 0.7 copy.16
  195.6 1.0 convert.4
  196.5 0.7 fusion.13
  (2 shorter events, 0.0 us)
Async XLA Ops:
  7.2 50.4 %all-gather.2.cloned.1.call-start = ((), (), s32[]{:S(2)}) async-start(), calls=%async_computation.1 | async-start | bytes 5677056 | tf_op jit(solution)/shard_map/all_gather | solution.py:326
  10.6 183.6 %reduce-scatter.2.cloned.1.call-start = ((), (), s32[]{:S(2)}) async-start(), calls=%async_computation.2 | async-start | bytes 11354112 | tf_op jit(solution)/shard_map/reduce_scatter | solution.py:328
Sparse Core Ops, SparseCore 0:
  10.8 46.7 all-gather.1
  93.9 100.2 reduce-scatter.1

commit v2 on v1

--- a/solution.py
+++ b/solution.py
@@ -297,6 +297,296 @@
     )(xd, w_gate, w_up, w_down)
 
 
+RING = 4
+NEAR = (0, -1, 1, 2)
+FAR = (2, -1, 1, 0)
+
+
+class Place:
+    def __init__(self):
+        self.at = {a: lax.axis_index(a) for a in GROUP_AXES}
+        self.size = {a: lax.axis_size(a) for a in GROUP_AXES}
+
+    def step(self, axis, d):
+        n = self.size[axis]
+        return lax.rem(self.at[axis] + (d + n), n)
+
+    def axes(self, m):
+        return ("col", "row") if m == 0 else ("row", "col")
+
+    def block(self, m, d1, d2, other):
+        ax1, ax2 = self.axes(m)
+        pos = {ax1: self.step(ax1, d1), ax2: self.step(ax2, d2)}
+        core = self.step("core", 1) if other else self.at["core"]
+        return (pos["row"] * self.size["col"] + pos["col"]) * self.size["core"] + core
+
+    def barrier(self):
+        sem = pltpu.get_barrier_semaphore()
+        peers = [{a: self.step(a, d)} for a in ("row", "col") for d in (-1, 1)] + [{"core": self.step("core", 1)}]
+        for peer in peers:
+            pl.semaphore_signal(sem, inc=1, device_id=peer, device_id_type=pl.DeviceIdType.MESH)
+        pl.semaphore_wait(sem, len(peers))
+
+
+def half_lanes(width):
+    mid = (width // LANES + 1) // 2 * LANES
+    return (pl.ds(0, mid), pl.ds(mid, width - mid))
+
+
+def gather_kernel(src_hbm, out_hbm, buf, send_sem, recv_sem, load_sem, out_sem):
+    here = Place()
+    width = src_hbm.shape[2]
+    halves = half_lanes(width)
+    sent = []
+
+    def move(m, idx, block, peer, lanes=None):
+        ref = buf.at[m, block] if lanes is None else buf.at[m, block, :, lanes]
+        return pltpu.make_async_remote_copy(src_ref=ref, dst_ref=ref, send_sem=send_sem.at[m, idx], recv_sem=recv_sem.at[m, idx],
+                                            device_id=peer, device_id_type=pl.DeviceIdType.MESH)
+
+    def send(m, idx, block, axis, d, lanes=None):
+        c = move(m, idx, block, {axis: here.step(axis, d)}, lanes)
+        c.start()
+        sent.append(c)
+
+    def arrive(m, idx, block, lanes=None):
+        move(m, idx, block, {"core": here.at["core"]}, lanes).wait_recv()
+
+    def keep(m, block):
+        pltpu.make_async_copy(buf.at[m, block], out_hbm.at[m, block], out_sem.at[m]).start()
+
+    def blk(m, i, d, other=False):
+        return here.block(m, NEAR[i], NEAR[d], other)
+
+    def have(m, i, d):
+        b = blk(m, i, d)
+        send(m, 20 + 4 * i + d, b, "core", 1)
+        keep(m, b)
+
+    def spread(m, i):
+        b = blk(m, i, 0)
+        ax2 = here.axes(m)[1]
+        send(m, 4 + 4 * i, b, ax2, 1)
+        send(m, 5 + 4 * i, b, ax2, -1)
+        have(m, i, 0)
+
+    loads = [pltpu.make_async_copy(src_hbm.at[m], buf.at[m, blk(m, 0, 0)], load_sem.at[m]) for m in range(2)]
+    for c in loads:
+        c.start()
+    here.barrier()
+    for m in range(2):
+        loads[m].wait()
+        ax1 = here.axes(m)[0]
+        send(m, 0, blk(m, 0, 0), ax1, 1)
+        send(m, 1, blk(m, 0, 0), ax1, -1)
+        spread(m, 0)
+
+    def first_axis(m):
+        ax1 = here.axes(m)[0]
+        arrive(m, 0, blk(m, 1, 0))
+        send(m, 2, blk(m, 1, 0), ax1, 1, halves[0])
+        spread(m, 1)
+        arrive(m, 1, blk(m, 2, 0))
+        send(m, 3, blk(m, 2, 0), ax1, -1, halves[1])
+        spread(m, 2)
+
+    def first_axis_far(m):
+        arrive(m, 2, blk(m, 3, 0), halves[0])
+        arrive(m, 3, blk(m, 3, 0), halves[1])
+        spread(m, 3)
+
+    def second_axis(m, i):
+        ax2 = here.axes(m)[1]
+        arrive(m, 4 + 4 * i, blk(m, i, 1))
+        send(m, 6 + 4 * i, blk(m, i, 1), ax2, 1, halves[0])
+        have(m, i, 1)
+        arrive(m, 5 + 4 * i, blk(m, i, 2))
+        send(m, 7 + 4 * i, blk(m, i, 2), ax2, -1, halves[1])
+        have(m, i, 2)
+
+    def second_axis_far(m, i):
+        arrive(m, 6 + 4 * i, blk(m, i, 3), halves[0])
+        arrive(m, 7 + 4 * i, blk(m, i, 3), halves[1])
+        have(m, i, 3)
+
+    for m in range(2):
+        first_axis(m)
+    for m in range(2):
+        second_axis(m, 0)
+    for m in range(2):
+        first_axis_far(m)
+    for m in range(2):
+        second_axis(m, 1)
+    for m in range(2):
+        second_axis_far(m, 0)
+        second_axis(m, 2)
+    for m in range(2):
+        second_axis_far(m, 1)
+        second_axis(m, 3)
+    for m in range(2):
+        second_axis_far(m, 2)
+    for m in range(2):
+        second_axis_far(m, 3)
+    for m in range(2):
+        for i in range(RING):
+            for d in range(RING):
+                b = blk(m, i, d, True)
+                arrive(m, 20 + 4 * i + d, b)
+                keep(m, b)
+    for c in sent:
+        c.wait_send()
+    for m in range(2):
+        pltpu.make_async_copy(buf.at[m], out_hbm.at[m], out_sem.at[m]).wait()
+
+
+def gather_tokens(packed, group):
+    _, tok_dev, width = packed.shape
+    full = (2, group, tok_dev, width)
+    sems = pltpu.SemaphoreType.DMA((2, 36))
+    return pl.pallas_call(
+        gather_kernel,
+        out_shape=jax.ShapeDtypeStruct(full, packed.dtype),
+        in_specs=[pl.BlockSpec(memory_space=pl.ANY)],
+        out_specs=pl.BlockSpec(memory_space=pl.ANY),
+        scratch_shapes=[pltpu.VMEM(full, packed.dtype), sems, sems, pltpu.SemaphoreType.DMA((2,)), pltpu.SemaphoreType.DMA((2,))],
+        compiler_params=pltpu.CompilerParams(collective_id=0, has_side_effects=True, vmem_limit_bytes=32_000_000),
+        name="gather_tokens",
+    )(packed)
+
+
+def reduce_kernel(dm, top_k, part_hbm, y_ref, dx_ref, dg_ref, own, pair, full, half, load_sem, pair_send, pair_recv, ring_send, ring_recv):
+    here = Place()
+    width = part_hbm.shape[3]
+    halves = half_lanes(width)
+    sent = []
+
+    def load(m, q):
+        b = here.block(m, FAR[q // RING], FAR[q % RING], False)
+        return pltpu.make_async_copy(part_hbm.at[m, b], own.at[m, q], load_sem.at[m, q])
+
+    def swap(m, q):
+        b = here.block(m, FAR[q // RING], FAR[q % RING], True)
+        return pltpu.make_async_remote_copy(src_ref=part_hbm.at[m, b], dst_ref=pair.at[m, q], send_sem=pair_send.at[m, q],
+                                            recv_sem=pair_recv.at[m, q], device_id={"core": here.step("core", 1)},
+                                            device_id_type=pl.DeviceIdType.MESH)
+
+    def ring(m, f, kind, q):
+        axis = here.axes(m)[0 if f == RING else 1]
+        d = 1 if kind % 2 == 0 else -1
+        if kind < 2:
+            src, dst = own.at[m, q, :, halves[kind]], half.at[m, f, :, halves[kind]]
+        else:
+            src, dst = own.at[m, q], full.at[m, f, kind - 2]
+        return pltpu.make_async_remote_copy(src_ref=src, dst_ref=dst, send_sem=ring_send.at[m, f, kind], recv_sem=ring_recv.at[m, f, kind],
+                                            device_id={axis: here.step(axis, d)}, device_id_type=pl.DeviceIdType.MESH)
+
+    def go(m, f, kind, q):
+        c = ring(m, f, kind, q)
+        c.start()
+        sent.append(c)
+
+    def at(f, d):
+        k = FAR.index(d)
+        return k * RING + FAR.index(0) if f == RING else f * RING + k
+
+    def add_pair(m, q):
+        load(m, q).wait()
+        swap(m, q).wait_recv()
+        own[m, q] = own[m, q] + pair[m, q]
+
+    def far(f, fresh):
+        for m in range(2):
+            if fresh:
+                add_pair(m, at(f, 2))
+        for m in range(2):
+            go(m, f, 0, at(f, 2))
+            go(m, f, 1, at(f, 2))
+
+    def near(f, fresh):
+        for m in range(2):
+            for kind, d in ((0, 1), (1, -1)):
+                q = at(f, d)
+                if fresh:
+                    add_pair(m, q)
+                ring(m, f, kind, q).wait_recv()
+                own[m, q, :, halves[kind]] = own[m, q, :, halves[kind]] + half[m, f, :, halves[kind]]
+        for m in range(2):
+            go(m, f, 2, at(f, 1))
+            go(m, f, 3, at(f, -1))
+
+    def done(f, fresh):
+        for m in range(2):
+            q = at(f, 0)
+            if fresh:
+                add_pair(m, q)
+            ring(m, f, 2, q).wait_recv()
+            ring(m, f, 3, q).wait_recv()
+            own[m, q] = own[m, q] + full[m, f, 0] + full[m, f, 1]
+
+    order = [at(0, 2), at(1, 2), at(0, 1), at(0, -1), at(2, 2), at(1, 1), at(1, -1), at(3, 2), at(2, 1), at(2, -1), at(0, 0),
+             at(3, 1), at(3, -1), at(1, 0), at(2, 0), at(3, 0)]
+    for q in order:
+        for m in range(2):
+            load(m, q).start()
+    here.barrier()
+    for q in order:
+        for m in range(2):
+            c = swap(m, q)
+            c.start()
+            sent.append(c)
+    far(0, True)
+    far(1, True)
+    near(0, True)
+    far(2, True)
+    near(1, True)
+    far(3, True)
+    near(2, True)
+    done(0, True)
+    far(RING, False)
+    near(3, True)
+    done(1, True)
+    done(2, True)
+    near(RING, False)
+    done(3, True)
+    done(RING, False)
+    q = at(RING, 0)
+    for m in range(2):
+        y_ref[m] = own[m, q, :, :dm].astype(BF16)
+        dx_ref[m] = own[m, q, :, dm:2 * dm].astype(BF16)
+        dg_ref[m] = own[m, q, :, 2 * dm:2 * dm + top_k]
+    for c in sent:
+        c.wait_send()
+
+
+def reduce_tokens(part, dm, top_k):
+    _, group, tok_dev, width = part.shape
+    chips = RING * RING
+    vmem = pl.BlockSpec(memory_space=pltpu.VMEM)
+    return pl.pallas_call(
+        functools.partial(reduce_kernel, dm, top_k),
+        out_shape=(
+            jax.ShapeDtypeStruct((2, tok_dev, dm), BF16),
+            jax.ShapeDtypeStruct((2, tok_dev, dm), BF16),
+            jax.ShapeDtypeStruct((2, tok_dev, top_k), F32),
+        ),
+        in_specs=[pl.BlockSpec(memory_space=pl.ANY)],
+        out_specs=(vmem, vmem, vmem),
+        scratch_shapes=[
+            pltpu.VMEM((2, chips, tok_dev, width), F32),
+            pltpu.VMEM((2, chips, tok_dev, width), F32),
+            pltpu.VMEM((2, RING + 1, 2, tok_dev, width), F32),
+            pltpu.VMEM((2, RING + 1, tok_dev, width), F32),
+            pltpu.SemaphoreType.DMA((2, chips)),
+            pltpu.SemaphoreType.DMA((2, chips)),
+            pltpu.SemaphoreType.DMA((2, chips)),
+            pltpu.SemaphoreType.DMA((2, RING + 1, 4)),
+            pltpu.SemaphoreType.DMA((2, RING + 1, 4)),
+        ],
+        compiler_params=pltpu.CompilerParams(collective_id=1, has_side_effects=True, vmem_limit_bytes=40_000_000),
+        name="reduce_tokens",
+    )(part)
+
+
 def pack_tokens(x, route_idx, gates, grad_y):
     def piece(v):
         return lax.reduce_precision(v, 8, 7)
@@ -323,12 +613,9 @@
         _, tok_dev, dm = x.shape
         top_k = route_idx.shape[2]
         packed = pack_tokens(x, route_idx, gates, grad_y)
-        xd = lax.all_gather(packed, GROUP_AXES, axis=1, tiled=True)
+        xd = gather_tokens(packed, group).reshape(2, group * tok_dev, packed.shape[2])
         part, g_gate, g_up, g_down = expert_stage(xd, w_gate, w_up, w_down, top_k, group * (tok_dev // 2))
-        mine = lax.psum_scatter(part, GROUP_AXES, scatter_dimension=1, tiled=True)
-        y = mine[:, :, :dm].astype(BF16)
-        dx = mine[:, :, dm:2 * dm].astype(BF16)
-        dg = mine[:, :, 2 * dm:2 * dm + top_k]
+        y, dx, dg = reduce_tokens(part.reshape(2, group, tok_dev, packed.shape[2]), dm, top_k)
         return y, dx, dg, g_gate, g_up, g_down
 
     return jax.shard_map(moe_layer, mesh=mesh, in_specs=(tok_spec, tok_spec, tok_spec, w_spec, w_spec, w_spec, tok_spec), out_specs=(tok_spec, tok_spec, tok_spec, w_spec, w_spec, w_spec), check_vma=False)

time: 205 us -> 135 us (0.66)
  waiting for transfers between devices: 147 us -> 0 us
  Pallas kernels: 36.1 us -> 122 us
  between operations: 14.1 us -> 0.68 us
  local copies, waits for them, and re-layouts: 3.62 us -> 9.97 us
    reduce_scatter x1 -> x0, waiting for transfers between devices: 100 us -> none  [moe_layer(): mine = lax.psum_scatter(part, GROUP_AXES, scatter_dimension=1, tiled=True)]
    pallas_call x0 -> x2, Pallas kernels: none -> 85.7 us  [the longest x1 53.9 us: reduce_tokens(): pl.pallas_call(functools.partial(reduce_kernel, dm, top_k), out_shape=(ja...]
    all_gather x1 -> x0, waiting for transfers between devices: 47 us -> none  [moe_layer(): xd = lax.all_gather(packed, GROUP_AXES, axis=1, tiled=True)]
    unnamed x3 -> x9, local copies, waits for them, and re-layouts: 2.22 us -> 9.97 us
  transfers between devices with their start and end apart: 2 -> 0, of which waited for: 2 -> 0; matrix products, arithmetic and copies ran while one was open for 0% -> 0% of each run, Pallas kernels for 0% -> 0%
where the time goes in v2:
time: 135 us; the launch traced here: 134 us
  Pallas kernels  122 us (90%)
  local copies, waits for them, and re-layouts  9.97 us (7%)
    pallas_call x1, Pallas kernels, reduce_tokens(): pl.pallas_call(functools.partial(reduce_kernel, dm, top_k), out_shape=(ja...  53.9 us
    pallas_call x1, Pallas kernels, expert_stage(): pl.pallas_call(functools.partial(expert_kernel, dims), out_shape=(jax.Sha...  36.2 us
    pallas_call x1, Pallas kernels, gather_tokens(): pl.pallas_call(gather_kernel, out_shape=jax.ShapeDtypeStruct(full, packed...  31.8 us
    unnamed x9, local copies, waits for them, and re-layouts  9.97 us

profile of v2, /device:TPU:97, one launch (start us, length us, event | category | flops | bytes accessed | tf_op | source)
XLA Modules:
  0.0 133.6 jit_solution(10735413408673519755)
XLA Ops:
  0.6 0.8 copy.13
  1.4 0.8 copy.14
  2.2 0.1 fusion.11
  2.3 0.9 fusion.1.src_hbm
  3.2 31.8 %gather_tokens.1 = bf16[2,32,16,2688]{3,2,1,0:T(8,128)(2,1)S(1)} custom-call(bf16[2,16,2688]{2,1,0:T(8,128)(2,1)S(1)} %fusion.1.src_hbm), custom_call_target="tpu_custom_call" | custom-call | tf_op jit(solution)/shard_map/gather_tokens/pallas_call | solution.py:446
  35.0 0.0 copy-start
  35.1 2.4 %copy-done = bf16[2,32,16,2688]{3,2,1,0:T(8,128)(2,1)} copy-done((bf16[2,32,16,2688]{3,2,1,0:T(8,128)(2,1)}, bf16[2,32,16,2688]{3,2,1,0:T(8,128)(2,1)S(1)}, u32[]{:S(2)}) %copy-start) | copy-done | bytes 5505048
  37.4 36.2 %experts.1 = (f32[2,512,2688]{2,1,0:T(8,128)}, f32[5,1280,384]{2,1,0:T(8,128)}, f32[5,1280,384]{2,1,0:T(8,128)}, f32[5,384,1280]{2,1,0:T(8,128)}) custom-call(bf16[2,512,2688]{2,1,0:T(8,128)(2,1)} %bitcast.2, bf16[5,1280,384]{2,1,0:T(8,128)(2,1)} %wg_hbm.1, bf16[5,1280,384]{2,1,0:T(8,128)(2,1)} %wu_hbm.1, bf16[5,384,1280]{2,1,0:T(8,128)(2,1)} %wd_hbm.1), custom_call_target="tpu_custom_call" | custom-call | tf_op jit(solution)/shard_map/experts/pallas_call | solution.py:262
  73.7 0.0 copy-start.1
  73.7 4.1 %copy-done.1 = f32[2,512,2688]{2,1,0:T(8,128)S(1)} copy-done((f32[2,512,2688]{2,1,0:T(8,128)S(1)}, f32[2,512,2688]{2,1,0:T(8,128)}, u32[]{:S(2)}) %copy-start.1) | copy-done | bytes 11010072
  77.8 53.9 %reduce_tokens.1 = (bf16[2,16,1280]{2,1,0:T(8,128)(2,1)S(1)}, bf16[2,16,1280]{2,1,0:T(8,128)(2,1)S(1)}, f32[2,16,6]{2,1,0:T(8,128)S(1)}) custom-call(f32[2,32,16,2688]{3,2,1,0:T(8,128)S(1)} %bitcast.3), custom_call_target="tpu_custom_call" | custom-call | tf_op jit(solution)/shard_map/reduce_tokens/pallas_call | solution.py:565
  131.7 0.7 copy.16
  132.4 0.6 copy.19
  133.0 0.6 copy.20
  (2 shorter events, 0.0 us)
Async XLA Ops:
  35.0 2.4 %copy-start = (bf16[2,32,16,2688]{3,2,1,0:T(8,128)(2,1)}, bf16[2,32,16,2688]{3,2,1,0:T(8,128)(2,1)S(1)}, u32[]{:S(2)}) copy-start(bf16[2,32,16,2688]{3,2,1,0:T(8,128)(2,1)S(1)} %gather_tokens.1) | copy-start | bytes 16515076
  73.7 4.1 %copy-start.1 = (f32[2,512,2688]{2,1,0:T(8,128)S(1)}, f32[2,512,2688]{2,1,0:T(8,128)}, u32[]{:S(2)}) copy-start(f32[2,512,2688]{2,1,0:T(8,128)} %get-tuple-element.13) | copy-start | bytes 33030148

commit v3 on v2

--- a/solution.py
+++ b/solution.py
@@ -255,7 +255,7 @@
 def expert_stage(xd, w_gate, w_up, w_down, top_k, seg):
     _, tokens, width = xd.shape
     el, dm, ff = w_gate.shape
-    any_spec = pl.BlockSpec(memory_space=pl.ANY)
+    any_spec = pl.BlockSpec(memory_space=pltpu.HBM)
     rows_max = el * seg
     tile_rows = seg + SMALL
     dims = (tokens, dm, ff, el, top_k, seg)
@@ -447,7 +447,7 @@
         gather_kernel,
         out_shape=jax.ShapeDtypeStruct(full, packed.dtype),
         in_specs=[pl.BlockSpec(memory_space=pl.ANY)],
-        out_specs=pl.BlockSpec(memory_space=pl.ANY),
+        out_specs=pl.BlockSpec(memory_space=pltpu.HBM),
         scratch_shapes=[pltpu.VMEM(full, packed.dtype), sems, sems, pltpu.SemaphoreType.DMA((2,)), pltpu.SemaphoreType.DMA((2,))],
         compiler_params=pltpu.CompilerParams(collective_id=0, has_side_effects=True, vmem_limit_bytes=32_000_000),
         name="gather_tokens",
@@ -569,7 +569,7 @@
             jax.ShapeDtypeStruct((2, tok_dev, dm), BF16),
             jax.ShapeDtypeStruct((2, tok_dev, top_k), F32),
         ),
-        in_specs=[pl.BlockSpec(memory_space=pl.ANY)],
+        in_specs=[pl.BlockSpec(memory_space=pltpu.HBM)],
         out_specs=(vmem, vmem, vmem),
         scratch_shapes=[
             pltpu.VMEM((2, chips, tok_dev, width), F32),

time: 135 us -> 134 us (level); the launches traced: 134 us -> 135 us
  no operation moved by 1% of the time
where the time goes in v3:
time: 134 us; the launch traced here: 135 us
  Pallas kernels  123 us (92%)
  local copies, waits for them, and re-layouts  9.97 us (7%)
    pallas_call x1, Pallas kernels, reduce_tokens(): pl.pallas_call(functools.partial(reduce_kernel, dm, top_k), out_shape=(ja...  55.1 us
    pallas_call x1, Pallas kernels, expert_stage(): pl.pallas_call(functools.partial(expert_kernel, dims), out_shape=(jax.Sha...  36.3 us
    pallas_call x1, Pallas kernels, gather_tokens(): pl.pallas_call(gather_kernel, out_shape=jax.ShapeDtypeStruct(full, packed...  31.8 us
    unnamed x9, local copies, waits for them, and re-layouts  9.97 us

profile of v3, /device:TPU:97, one launch (start us, length us, event | category | flops | bytes accessed | tf_op | source)
XLA Modules:
  0.0 134.9 jit_solution(10735413408673519755)
XLA Ops:
  0.6 0.8 copy.13
  1.4 0.8 copy.14
  2.2 0.1 fusion.11
  2.3 0.9 fusion.1.src_hbm
  3.2 31.8 %gather_tokens.1 = bf16[2,32,16,2688]{3,2,1,0:T(8,128)(2,1)S(1)} custom-call(bf16[2,16,2688]{2,1,0:T(8,128)(2,1)S(1)} %fusion.1.src_hbm), custom_call_target="tpu_custom_call" | custom-call | tf_op jit(solution)/shard_map/gather_tokens/pallas_call | solution.py:446
  35.0 0.0 copy-start
  35.1 2.4 %copy-done = bf16[2,32,16,2688]{3,2,1,0:T(8,128)(2,1)} copy-done((bf16[2,32,16,2688]{3,2,1,0:T(8,128)(2,1)}, bf16[2,32,16,2688]{3,2,1,0:T(8,128)(2,1)S(1)}, u32[]{:S(2)}) %copy-start) | copy-done | bytes 5505048
  37.4 36.3 %experts.1 = (f32[2,512,2688]{2,1,0:T(8,128)}, f32[5,1280,384]{2,1,0:T(8,128)}, f32[5,1280,384]{2,1,0:T(8,128)}, f32[5,384,1280]{2,1,0:T(8,128)}) custom-call(bf16[2,512,2688]{2,1,0:T(8,128)(2,1)} %bitcast.2, bf16[5,1280,384]{2,1,0:T(8,128)(2,1)} %wg_hbm.1, bf16[5,1280,384]{2,1,0:T(8,128)(2,1)} %wu_hbm.1, bf16[5,384,1280]{2,1,0:T(8,128)(2,1)} %wd_hbm.1), custom_call_target="tpu_custom_call" | custom-call | tf_op jit(solution)/shard_map/experts/pallas_call | solution.py:262
  73.7 0.0 copy-start.1
  73.7 4.1 %copy-done.1 = f32[2,512,2688]{2,1,0:T(8,128)S(1)} copy-done((f32[2,512,2688]{2,1,0:T(8,128)S(1)}, f32[2,512,2688]{2,1,0:T(8,128)}, u32[]{:S(2)}) %copy-start.1) | copy-done | bytes 11010072
  77.8 55.1 %reduce_tokens.1 = (bf16[2,16,1280]{2,1,0:T(8,128)(2,1)S(1)}, bf16[2,16,1280]{2,1,0:T(8,128)(2,1)S(1)}, f32[2,16,6]{2,1,0:T(8,128)S(1)}) custom-call(f32[2,32,16,2688]{3,2,1,0:T(8,128)S(1)} %bitcast.3), custom_call_target="tpu_custom_call" | custom-call | tf_op jit(solution)/shard_map/reduce_tokens/pallas_call | solution.py:565
  132.9 0.7 copy.16
  133.6 0.6 copy.19
  134.2 0.6 copy.20
  (2 shorter events, 0.0 us)
Async XLA Ops:
  35.0 2.4 %copy-start = (bf16[2,32,16,2688]{3,2,1,0:T(8,128)(2,1)}, bf16[2,32,16,2688]{3,2,1,0:T(8,128)(2,1)S(1)}, u32[]{:S(2)}) copy-start(bf16[2,32,16,2688]{3,2,1,0:T(8,128)(2,1)S(1)} %gather_tokens.1) | copy-start | bytes 16515076
  73.7 4.1 %copy-start.1 = (f32[2,512,2688]{2,1,0:T(8,128)S(1)}, f32[2,512,2688]{2,1,0:T(8,128)}, u32[]{:S(2)}) copy-start(f32[2,512,2688]{2,1,0:T(8,128)} %get-tuple-element.13) | copy-start | bytes 33030148

commit v4 on v1

--- a/solution.py
+++ b/solution.py
@@ -13,6 +13,7 @@
 BF16 = jnp.bfloat16
 LANES = 128
 SMALL = 32
+VMEM_LIMIT = 66_000_000
 
 
 def dot_nn(a, b):
@@ -255,7 +256,7 @@
 def expert_stage(xd, w_gate, w_up, w_down, top_k, seg):
     _, tokens, width = xd.shape
     el, dm, ff = w_gate.shape
-    any_spec = pl.BlockSpec(memory_space=pl.ANY)
+    any_spec = pl.BlockSpec(memory_space=pltpu.HBM)
     rows_max = el * seg
     tile_rows = seg + SMALL
     dims = (tokens, dm, ff, el, top_k, seg)
@@ -292,26 +293,299 @@
             pltpu.SemaphoreType.DMA((2, 3)),
             pltpu.SemaphoreType.DMA((2,)),
         ],
-        compiler_params=pltpu.CompilerParams(vmem_limit_bytes=66_000_000),
+        compiler_params=pltpu.CompilerParams(vmem_limit_bytes=VMEM_LIMIT),
         name="experts",
     )(xd, w_gate, w_up, w_down)
 
 
-def pack_tokens(x, route_idx, gates, grad_y):
-    def piece(v):
-        return lax.reduce_precision(v, 8, 7)
-
-    g1 = piece(gates)
-    g2 = piece(gates - g1)
-    g3 = piece(gates - g1 - g2)
-
-    def pad(v):
-        return jnp.pad(v.astype(BF16), ((0, 0), (0, 0), (0, 8 - v.shape[2])))
-
-    ids = route_idx.astype(F32)
-    meta = jnp.concatenate([pad(ids), pad(g1), pad(g2), pad(g3)], axis=2)
-    meta = jnp.pad(meta, ((0, 0), (0, 0), (0, LANES - meta.shape[2])))
-    return jnp.concatenate([x, grad_y, meta], axis=2)
+RING = 4
+NEAR = (0, -1, 1, 2)
+FAR = (2, -1, 1, 0)
+GROUPS = (slice(0, 1), slice(1, 3), slice(3, 4))
+MESH = pl.DeviceIdType.MESH
+
+
+class Place:
+    def __init__(self):
+        self.row, self.col, self.core = (lax.axis_index(a) for a in GROUP_AXES)
+        self.n_row, self.n_col = lax.axis_size("row"), lax.axis_size("col")
+        self.other = 1 - self.core
+        self.partner = {"core": self.other}
+
+    def spot(self, first, d1, d2):
+        row = lax.rem(self.row + (d1 * first + d2 * (1 - first)) + self.n_row, self.n_row)
+        col = lax.rem(self.col + (d1 * (1 - first) + d2 * first) + self.n_col, self.n_col)
+        return row, col
+
+    def chip(self, first, d1, d2):
+        row, col = self.spot(first, d1, d2)
+        return row * self.n_col + col
+
+    def peer(self, axis, d):
+        row, col = self.spot(self.core, d, 0) if axis == 1 else self.spot(self.core, 0, d)
+        return {"row": row, "col": col}
+
+    def barrier(self):
+        sem = pltpu.get_barrier_semaphore()
+        peers = [self.peer(axis, d) for axis in (1, 2) for d in (1, -1)] + [self.partner]
+        for peer in peers:
+            pl.semaphore_signal(sem, inc=1, device_id=peer, device_id_type=MESH)
+        pl.semaphore_wait(sem, len(peers))
+
+
+def half_lanes(width):
+    mid = (width // LANES + 1) // 2 * LANES
+    return (pl.ds(0, mid), pl.ds(mid, width - mid))
+
+
+def token_meta(route, gates):
+    top_k, tok_dev = route.shape
+    zero = jnp.zeros((8 - top_k, tok_dev), F32)
+    parts = [route.astype(F32)] + [p.astype(F32) for p in split3(gates)]
+    rows = jnp.concatenate([v for p in parts for v in (p, zero)], axis=0).astype(BF16)
+    n = rows.shape[0]
+    eye = (lax.broadcasted_iota(jnp.int32, (n, LANES), 0) == lax.broadcasted_iota(jnp.int32, (n, LANES), 1)).astype(F32).astype(BF16)
+    return dot_tn(rows, eye).astype(BF16)
+
+
+def gather_kernel(x_hbm, dy_hbm, route_ref, gates_ref, out_hbm, buf, stage, send_sem, recv_sem, load_sem, out_sem):
+    here = Place()
+    k, other = here.core, here.other
+    dm = x_hbm.shape[2]
+    halves = half_lanes(2 * dm + LANES)
+    sent = []
+
+    def move(idx, src, dst, peer):
+        return pltpu.make_async_remote_copy(src_ref=src, dst_ref=dst, send_sem=send_sem.at[idx], recv_sem=recv_sem.at[idx],
+                                            device_id=peer, device_id_type=MESH)
+
+    def send(idx, src, dst, peer):
+        c = move(idx, src, dst, peer)
+        c.start()
+        sent.append(c)
+
+    def arrive(idx, dst):
+        move(idx, dst, dst, here.partner).wait_recv()
+
+    def keep(mine, g, d):
+        first = k if mine else other
+        for i in range(g.start, g.stop):
+            c = here.chip(first, NEAR[i], NEAR[d])
+            pltpu.make_async_copy(buf.at[0 if mine else 1, d, i], out_hbm.at[first, c], out_sem.at[0 if mine else 1]).start()
+
+    def have(gi, d):
+        g = GROUPS[gi]
+        send(17 + 3 * d + gi, buf.at[0, d, g], buf.at[1, d, g], here.partner)
+        keep(True, g, d)
+
+    def spread(gi):
+        g = GROUPS[gi]
+        send(5 + 4 * gi, buf.at[0, 0, g], buf.at[0, 1, g], here.peer(2, 1))
+        send(6 + 4 * gi, buf.at[0, 0, g], buf.at[0, 2, g], here.peer(2, -1))
+        have(gi, 0)
+
+    def second(gi):
+        g = GROUPS[gi]
+        for d, step in ((1, 1), (2, -1)):
+            arrive(4 + 4 * gi + d, buf.at[0, d, g])
+            lanes = halves[d - 1]
+            send(6 + 4 * gi + d, buf.at[0, d, g, :, :, lanes], buf.at[0, 3, g, :, :, lanes], here.peer(2, step))
+            have(gi, d)
+
+    def second_far(gi):
+        g = GROUPS[gi]
+        for d in (1, 2):
+            arrive(6 + 4 * gi + d, buf.at[0, 3, g, :, :, halves[d - 1]])
+        have(gi, 3)
+
+    mine = buf.at[0, 0, 0, k]
+    loads = [pltpu.make_async_copy(h.at[mb], dst.at[:, pl.ds(lo, dm)], load_sem.at[n])
+             for n, (h, mb, dst, lo) in enumerate(((x_hbm, other, stage, 0), (dy_hbm, other, stage, dm), (x_hbm, k, mine, 0), (dy_hbm, k, mine, dm)))]
+    for c in loads:
+        c.start()
+    metas = [token_meta(route_ref[:, m, :], gates_ref[:, m, :]) for m in range(2)]
+    zero_core = k == 0
+    stage[:, 2 * dm:] = jnp.where(zero_core, metas[1].astype(F32), metas[0].astype(F32)).astype(BF16)
+    buf[0, 0, 0, k, :, 2 * dm:] = jnp.where(zero_core, metas[0].astype(F32), metas[1].astype(F32)).astype(BF16)
+    here.barrier()
+    for c in loads:
+        c.wait()
+    send(0, stage, buf.at[0, 0, 0, k], here.partner)
+    arrive(0, buf.at[0, 0, 0, other])
+    send(1, buf.at[0, 0, 0], buf.at[0, 0, 1], here.peer(1, 1))
+    send(2, buf.at[0, 0, 0], buf.at[0, 0, 2], here.peer(1, -1))
+    spread(0)
+    arrive(1, buf.at[0, 0, 1])
+    send(3, buf.at[0, 0, 1, :, :, halves[0]], buf.at[0, 0, 3, :, :, halves[0]], here.peer(1, 1))
+    arrive(2, buf.at[0, 0, 2])
+    send(4, buf.at[0, 0, 2, :, :, halves[1]], buf.at[0, 0, 3, :, :, halves[1]], here.peer(1, -1))
+    spread(1)
+    second(0)
+    arrive(3, buf.at[0, 0, 3, :, :, halves[0]])
+    arrive(4, buf.at[0, 0, 3, :, :, halves[1]])
+    spread(2)
+    second(1)
+    second_far(0)
+    second(2)
+    second_far(1)
+    second_far(2)
+    for gi, d in [(gi, d) for d in range(RING) for gi in range(len(GROUPS))]:
+        arrive(17 + 3 * d + gi, buf.at[1, d, GROUPS[gi]])
+        keep(False, GROUPS[gi], d)
+    for c in sent:
+        c.wait_send()
+    for n, mb in enumerate((k, other)):
+        pltpu.make_async_copy(out_hbm.at[mb], out_hbm.at[mb], out_sem.at[n]).wait()
+
+
+def gather_tokens(x, grad_y, route_idx, gates, chips):
+    _, tok_dev, dm = x.shape
+    width = 2 * dm + LANES
+    hbm = pl.BlockSpec(memory_space=pltpu.HBM)
+    vmem = pl.BlockSpec(memory_space=pltpu.VMEM)
+    sems = pltpu.SemaphoreType.DMA((29,))
+    return pl.pallas_call(
+        gather_kernel,
+        out_shape=jax.ShapeDtypeStruct((2, chips, 2, tok_dev, width), BF16),
+        in_specs=[hbm, hbm, vmem, vmem],
+        out_specs=hbm,
+        scratch_shapes=[pltpu.VMEM((2, RING, RING, 2, tok_dev, width), BF16), pltpu.VMEM((tok_dev, width), BF16),
+                        sems, sems, pltpu.SemaphoreType.DMA((4,)), pltpu.SemaphoreType.DMA((2,))],
+        compiler_params=pltpu.CompilerParams(collective_id=0, has_side_effects=True, vmem_limit_bytes=VMEM_LIMIT),
+        name="gather_tokens",
+    )(x, grad_y, jnp.transpose(route_idx, (2, 0, 1)), jnp.transpose(gates, (2, 0, 1)))
+
+
+def reduce_kernel(dm, top_k, part_hbm, y_ref, dx_ref, dg_ref, own, pair, full, half, last, load_sem, pair_send, pair_recv,
+                  ring_send, ring_recv, last_sem):
+    here = Place()
+    k, other = here.core, here.other
+    halves = half_lanes(part_hbm.shape[4])
+    sent = []
+
+    def load(d, i):
+        return pltpu.make_async_copy(part_hbm.at[k, here.chip(k, FAR[i], FAR[d])], own.at[d, i], load_sem.at[d, i])
+
+    def swap(d, i):
+        return pltpu.make_async_remote_copy(src_ref=part_hbm.at[other, here.chip(other, FAR[i], FAR[d])], dst_ref=pair.at[d, i],
+                                            send_sem=pair_send.at[d, i], recv_sem=pair_recv.at[d, i], device_id=here.partner, device_id_type=MESH)
+
+    def move(f, kind, src, dst, axis):
+        return pltpu.make_async_remote_copy(src_ref=src, dst_ref=dst, send_sem=ring_send.at[f, kind], recv_sem=ring_recv.at[f, kind],
+                                            device_id=here.peer(axis, 1 if kind % 2 == 0 else -1), device_id_type=MESH)
+
+    def go(f, kind, src, dst, axis):
+        c = move(f, kind, src, dst, axis)
+        c.start()
+        sent.append(c)
+
+    def arrive(f, kind, dst):
+        move(f, kind, dst, dst, 1).wait_recv()
+
+    def add_pair(d, gi):
+        for i in range(GROUPS[gi].start, GROUPS[gi].stop):
+            load(d, i).wait()
+            swap(d, i).wait_recv()
+            own[d, i] = own[d, i] + pair[d, i]
+
+    def far(f, src, g, axis):
+        for kind in range(2):
+            go(f, kind, src.at[:, :, :, halves[kind]], half.at[g, :, :, halves[kind]], axis)
+
+    def near(f, ref, g, axis):
+        for kind, step in ((0, 1), (1, -1)):
+            lanes = halves[kind]
+            arrive(f, kind, half.at[g, :, :, lanes])
+            d, at = ref(step)
+            own[d, at, :, :, lanes] = own[d, at, :, :, lanes] + half[g, :, :, lanes]
+        for kind, step in ((2, 1), (3, -1)):
+            d, at = ref(step)
+            go(f, kind, own.at[d, at], full.at[kind - 2, g], axis)
+
+    def done(f, at, g):
+        arrive(f, 2, full.at[0, g])
+        arrive(f, 3, full.at[1, g])
+        own[3, at] = own[3, at] + full[0, g] + full[1, g]
+
+    def far2(gi):
+        add_pair(0, gi)
+        far(gi, own.at[0, GROUPS[gi]], GROUPS[gi], 2)
+
+    def near2(gi):
+        add_pair(2, gi)
+        add_pair(1, gi)
+        near(gi, lambda step: (2 if step == 1 else 1, GROUPS[gi]), GROUPS[gi], 2)
+
+    def done2(gi):
+        add_pair(3, gi)
+        done(gi, GROUPS[gi], GROUPS[gi])
+
+    order = [(0, 0), (0, 1), (0, 2), (2, 0), (1, 0), (0, 3), (2, 1), (2, 2), (1, 1), (1, 2), (3, 0), (2, 3), (1, 3), (3, 1), (3, 2), (3, 3)]
+    for q in order:
+        load(*q).start()
+    here.barrier()
+    for q in order:
+        c = swap(*q)
+        c.start()
+        sent.append(c)
+    lone = slice(RING, RING + 1)
+    far2(0)
+    far2(1)
+    near2(0)
+    far2(2)
+    near2(1)
+    done2(0)
+    far(3, own.at[3, slice(0, 1)], lone, 1)
+    near2(2)
+    done2(1)
+    near(3, lambda step: (3, slice(2, 3) if step == 1 else slice(1, 2)), lone, 1)
+    done2(2)
+    done(3, slice(3, 4), lone)
+
+    give = pltpu.make_async_remote_copy(src_ref=own.at[3, 3, other], dst_ref=last, send_sem=last_sem.at[0], recv_sem=last_sem.at[1],
+                                        device_id=here.partner, device_id_type=MESH)
+    give.start()
+    sent.append(give)
+
+    def emit(mb, val):
+        y_ref[mb] = val[:, :dm].astype(BF16)
+        dx_ref[mb] = val[:, dm:2 * dm].astype(BF16)
+        dg_ref[mb] = val[:, 2 * dm:2 * dm + top_k]
+
+    emit(k, own[3, 3, k])
+    give.wait_recv()
+    emit(other, last[...])
+    for c in sent:
+        c.wait_send()
+
+
+def reduce_tokens(part, dm, top_k):
+    _, chips, cores, tok_dev, width = part.shape
+    vmem = pl.BlockSpec(memory_space=pltpu.VMEM)
+    block = (cores, tok_dev, width)
+    ring_sems = pltpu.SemaphoreType.DMA((4, 4))
+    pair_sems = pltpu.SemaphoreType.DMA((RING, RING))
+    return pl.pallas_call(
+        functools.partial(reduce_kernel, dm, top_k),
+        out_shape=(
+            jax.ShapeDtypeStruct((2, tok_dev, dm), BF16),
+            jax.ShapeDtypeStruct((2, tok_dev, dm), BF16),
+            jax.ShapeDtypeStruct((2, tok_dev, top_k), F32),
+        ),
+        in_specs=[pl.BlockSpec(memory_space=pltpu.HBM)],
+        out_specs=(vmem, vmem, vmem),
+        scratch_shapes=[
+            pltpu.VMEM((RING, RING) + block, F32),
+            pltpu.VMEM((RING, RING) + block, F32),
+            pltpu.VMEM((2, RING + 1) + block, F32),
+            pltpu.VMEM((RING + 1,) + block, F32),
+            pltpu.VMEM((tok_dev, width), F32),
+            pair_sems, pair_sems, pair_sems, ring_sems, ring_sems,
+            pltpu.SemaphoreType.DMA((2,)),
+        ],
+        compiler_params=pltpu.CompilerParams(collective_id=1, has_side_effects=True, vmem_limit_bytes=VMEM_LIMIT),
+        name="reduce_tokens",
+    )(part)
 
 
 def solution(mesh):
@@ -322,13 +596,11 @@
     def moe_layer(x, route_idx, gates, w_gate, w_up, w_down, grad_y):
         _, tok_dev, dm = x.shape
         top_k = route_idx.shape[2]
-        packed = pack_tokens(x, route_idx, gates, grad_y)
-        xd = lax.all_gather(packed, GROUP_AXES, axis=1, tiled=True)
+        width = 2 * dm + LANES
+        chips = group // 2
+        xd = gather_tokens(x, grad_y, route_idx, gates, chips).reshape(2, group * tok_dev, width)
         part, g_gate, g_up, g_down = expert_stage(xd, w_gate, w_up, w_down, top_k, group * (tok_dev // 2))
-        mine = lax.psum_scatter(part, GROUP_AXES, scatter_dimension=1, tiled=True)
-        y = mine[:, :, :dm].astype(BF16)
-        dx = mine[:, :, dm:2 * dm].astype(BF16)
-        dg = mine[:, :, 2 * dm:2 * dm + top_k]
+        y, dx, dg = reduce_tokens(part.reshape(2, chips, 2, tok_dev, width), dm, top_k)
         return y, dx, dg, g_gate, g_up, g_down
 
     return jax.shard_map(moe_layer, mesh=mesh, in_specs=(tok_spec, tok_spec, tok_spec, w_spec, w_spec, w_spec, tok_spec), out_specs=(tok_spec, tok_spec, tok_spec, w_spec, w_spec, w_spec), check_vma=False)

time: 205 us -> 120 us (0.59)
  waiting for transfers between devices: 147 us -> 0 us
  Pallas kernels: 36.1 us -> 116 us
  between operations: 14.1 us -> 0.66 us
  other arithmetic: 2.71 us -> 0 us
    reduce_scatter x1 -> x0, waiting for transfers between devices: 100 us -> none  [moe_layer(): mine = lax.psum_scatter(part, GROUP_AXES, scatter_dimension=1, tiled=True)]
    pallas_call x0 -> x2, Pallas kernels: none -> 79.6 us  [the longest x1 49 us: reduce_tokens(): pl.pallas_call(functools.partial(reduce_kernel, dm, top_k), out_shape=(ja...]
    all_gather x1 -> x0, waiting for transfers between devices: 47 us -> none  [moe_layer(): xd = lax.all_gather(packed, GROUP_AXES, axis=1, tiled=True)]
    unnamed x3, local copies, waits for them, and re-layouts: 2.22 us -> 4.44 us
  transfers between devices with their start and end apart: 2 -> 0, of which waited for: 2 -> 0; matrix products, arithmetic and copies ran while one was open for 0% -> 0% of each run, Pallas kernels for 0% -> 0%
where the time goes in v4:
time: 120 us; the launch traced here: 121 us
  Pallas kernels  116 us (97%)
  local copies, waits for them, and re-layouts  4.44 us (4%)
    pallas_call x1, Pallas kernels, reduce_tokens(): pl.pallas_call(functools.partial(reduce_kernel, dm, top_k), out_shape=(ja...  49 us
    pallas_call x1, Pallas kernels, expert_stage(): pl.pallas_call(functools.partial(expert_kernel, dims), out_shape=(jax.Sha...  36.2 us
    pallas_call x1, Pallas kernels, gather_tokens(): pl.pallas_call(gather_kernel, out_shape=jax.ShapeDtypeStruct((2, chips, 2...  30.6 us
    unnamed x3, local copies, waits for them, and re-layouts  4.44 us

profile of v4, /device:TPU:97, one launch (start us, length us, event | category | flops | bytes accessed | tf_op | source)
XLA Modules:
  0.0 120.9 jit_solution(1886425509395593023)
XLA Ops:
  0.6 30.6 %gather_tokens.1 = bf16[2,16,2,16,2688]{4,3,2,1,0:T(8,128)(2,1)} custom-call(bf16[2,16,1280]{2,1,0:T(8,128)(2,1)} %x_hbm.1, bf16[2,16,1280]{2,1,0:T(8,128)(2,1)} %dy_hbm.1, s32[6,2,16]{2,1,0:T(2,128)} %bitcast.6, f32[6,2,16]{2,1,0:T(2,128)} %bitcast.7), custom_call_target="tpu_custom_call" | custom-call | tf_op jit(solution)/shard_map/gather_tokens/pallas_call | solution.py:447
  31.2 36.2 %experts.1 = (f32[2,512,2688]{2,1,0:T(8,128)}, f32[5,1280,384]{2,1,0:T(8,128)}, f32[5,1280,384]{2,1,0:T(8,128)}, f32[5,384,1280]{2,1,0:T(8,128)}) custom-call(bf16[2,512,2688]{2,1,0:T(8,128)(2,1)} %bitcast.4, bf16[5,1280,384]{2,1,0:T(8,128)(2,1)} %wg_hbm.1, bf16[5,1280,384]{2,1,0:T(8,128)(2,1)} %wu_hbm.1, bf16[5,384,1280]{2,1,0:T(8,128)(2,1)} %wd_hbm.1), custom_call_target="tpu_custom_call" | custom-call | tf_op jit(solution)/shard_map/experts/pallas_call | solution.py:263
  67.5 49.0 %reduce_tokens.1 = (bf16[2,16,1280]{2,1,0:T(8,128)(2,1)}, bf16[2,16,1280]{2,1,0:T(8,128)(2,1)}, f32[2,16,6]{2,1,0:T(8,128)}) custom-call(f32[2,16,2,16,2688]{4,3,2,1,0:T(8,128)} %bitcast.5), custom_call_target="tpu_custom_call" | custom-call | tf_op jit(solution)/shard_map/reduce_tokens/pallas_call | solution.py:568
  116.5 1.4 %copy.13 = f32[2,16,6]{1,0,2:T(2,128)} copy(f32[2,16,6]{2,1,0:T(8,128)} %get-tuple-element.22) | data formatting | bytes 1536
  117.9 1.5 %copy.16 = bf16[2,16,1280]{2,1,0:T(8,128)(2,1)} copy(bf16[2,16,1280]{2,1,0:T(8,128)(2,1)} %get-tuple-element.32) | data formatting | bytes 163840
  119.4 1.5 %copy.17 = bf16[2,16,1280]{2,1,0:T(8,128)(2,1)} copy(bf16[2,16,1280]{2,1,0:T(8,128)(2,1)} %get-tuple-element.33) | data formatting | bytes 163840

commit v5 on v4

--- a/solution.py
+++ b/solution.py
@@ -41,7 +41,7 @@
 
 
 def expert_kernel(dims, xd_hbm, wg_hbm, wu_hbm, wd_hbm, part_hbm, gg_hbm, gu_hbm, gd_hbm,
-                  xd_v, pt_v, gr_v, acc_v, wg_v, wu_v, wd_v, og_v, ou_v, od_v, pos_v,
+                  xd_v, pt_v, gr_v, acc_v, wgu_v, wd_v, og_v, ou_v, od_v, pos_v,
                   xt_v, qt_v, a_v, duv_v, cnt_s, base_s, sem_x, sem_w, sem_o, sem_p):
     tokens, dm, ff, el, top_k, seg = dims
     n_row, n_col, n_core = lax.axis_size("row"), lax.axis_size("col"), lax.axis_size("core")
@@ -49,8 +49,8 @@
     width = 2 * dm + LANES
 
     def load_w(e, slot):
-        return [pltpu.make_async_copy(h.at[e], v.at[slot], sem_w.at[slot, i])
-                for i, (h, v) in enumerate(((wg_hbm, wg_v), (wu_hbm, wu_v), (wd_hbm, wd_v)))]
+        pairs = ((wg_hbm, wgu_v.at[slot, :, pl.ds(0, ff)]), (wu_hbm, wgu_v.at[slot, :, pl.ds(ff, ff)]), (wd_hbm, wd_v.at[slot]))
+        return [pltpu.make_async_copy(h.at[e], v, sem_w.at[slot, i]) for i, (h, v) in enumerate(pairs)]
 
     def store_g(e, slot):
         return [pltpu.make_async_copy(v.at[slot], h.at[e], sem_o.at[slot, i])
@@ -59,9 +59,6 @@
     loads_x = [pltpu.make_async_copy(xd_hbm.at[m], xd_v.at[m], sem_x.at[m]) for m in range(2)]
     for c in loads_x:
         c.start()
-    for s in range(2):
-        for c in load_w(s, s):
-            c.start()
 
     row_i = lax.broadcasted_iota(jnp.int32, (tokens, tokens), 0)
     col_i = lax.broadcasted_iota(jnp.int32, (tokens, tokens), 1)
@@ -75,6 +72,8 @@
     n_chunks = []
     for m in range(2):
         loads_x[m].wait()
+        for c in load_w(m, m):
+            c.start()
         meta_t = xd_v[m, :, 2 * dm:].astype(F32).T
         hits = jnp.zeros((8, tokens), F32)
         for j in range(top_k):
@@ -119,10 +118,7 @@
         def write(s, w, val):
             merged = jnp.where(valid, val.astype(F32), read(s, w).astype(F32)).astype(BF16)
             gr_v[m_a, pl.ds(base_a, ra), s:s + w] = merged[:ra]
-
-            @pl.when(n_b > 0)
-            def _():
-                gr_v[1 - m_a, pl.ds(base_b, rb), s:s + w] = merged[ra:]
+            gr_v[1 - m_a, pl.ds(base_b, rb), s:s + w] = merged[ra:]
 
         lane = lax.broadcasted_iota(jnp.int32, (rows, LANES), 1)
         meta = jnp.where(valid, read(2 * dm, LANES).astype(F32), 0.0)
@@ -135,16 +131,15 @@
             dy = jnp.where(valid, read(dm + s, w).astype(F32), 0.0)
             qt_v[:rows, s:s + w] = (gate * dy).astype(BF16)
         xt = xt_v[:rows, :]
-        u = dot_nn(xt, wg_v[slot]).astype(BF16).astype(F32)
-        v = dot_nn(xt, wu_v[slot]).astype(BF16).astype(F32)
+        uv = dot_nn(xt, wgu_v[slot]).astype(BF16).astype(F32)
+        u, v = uv[:, :ff], uv[:, ff:]
         r = dot_nt(qt_v[:rows, :], wd_v[slot])
         s_g = jax.nn.sigmoid(u)
         a_v[:rows, :] = (u * s_g * v).astype(BF16)
         duv_v[:rows, :ff] = (r * v * s_g * (1.0 + u * (1.0 - s_g))).astype(BF16)
         duv_v[:rows, ff:] = (r * u * s_g).astype(BF16)
         a = a_v[:rows, :]
-        du = duv_v[:rows, :ff]
-        dv = duv_v[:rows, ff:]
+        duv = duv_v[:rows, :]
         dots = jnp.zeros((rows, 1), F32)
         for s, w in col_blocks(dm, 256):
             o = dot_nn(a, wd_v[slot, :, s:s + w]).astype(BF16)
@@ -152,8 +147,7 @@
             dots = dots + jnp.sum(dy * o.astype(F32), axis=1, keepdims=True)
             write(s, w, o)
         for s, w in col_blocks(dm, 256):
-            p = dot_nt(du, wg_v[slot, s:s + w, :]) + dot_nt(dv, wu_v[slot, s:s + w, :])
-            write(dm + s, w, p.astype(BF16))
+            write(dm + s, w, dot_nt(duv, wgu_v[slot, s:s + w, :]).astype(BF16))
         d1, d2, d3 = split3(dots)
         g1, g2, g3 = split3(gate)
         new_meta = jnp.zeros((rows, LANES), F32)
@@ -167,7 +161,6 @@
             else:
                 ref[idx] = jnp.where(first, 0.0, ref[idx]) + val
 
-        duv = duv_v[:rows, :]
         for s, w in col_blocks(dm, 256):
             g_in = dot_tn(xt_v[:rows, s:s + w], duv)
             put(og_v, (slot, slice(s, s + w)), g_in[:, :ff])
@@ -275,8 +268,7 @@
             pltpu.VMEM((2, tokens, rows_max), BF16),
             pltpu.VMEM((2, rows_max, width), BF16),
             pltpu.VMEM((2, tokens, width), F32),
-            pltpu.VMEM((2, dm, ff), BF16),
-            pltpu.VMEM((2, dm, ff), BF16),
+            pltpu.VMEM((2, dm, 2 * ff), BF16),
             pltpu.VMEM((2, ff, dm), BF16),
             pltpu.VMEM((2, dm, ff), F32),
             pltpu.VMEM((2, dm, ff), F32),
@@ -375,27 +367,46 @@
 
     def have(gi, d):
         g = GROUPS[gi]
-        send(17 + 3 * d + gi, buf.at[0, d, g], buf.at[1, d, g], here.partner)
+        send(24 + 3 * d + gi, buf.at[0, d, g], buf.at[1, d, g], here.partner)
         keep(True, g, d)
 
+    def both_ways(p, src, left, right, axis):
+        for way, dst in ((0, left), (1, right)):
+            for n in range(2):
+                lanes = halves[way if n == 0 else 1 - way]
+                send(6 * p + 2 * way + n, src.at[:, :, :, lanes], dst.at[:, :, :, lanes], here.peer(axis, 1 - 2 * way))
+
+    def relay(p, left, right, far, axis):
+        for way, src in ((0, left), (1, right)):
+            lanes = halves[way]
+            arrive(6 * p + 2 * way, src.at[:, :, :, lanes])
+            send(6 * p + 4 + way, src.at[:, :, :, lanes], far.at[:, :, :, lanes], here.peer(axis, 1 - 2 * way))
+
+    def rest(p, left, right):
+        for way, src in ((0, left), (1, right)):
+            arrive(6 * p + 2 * way + 1, src.at[:, :, :, halves[1 - way]])
+
+    def far_end(p, far):
+        for way in range(2):
+            arrive(6 * p + 4 + way, far.at[:, :, :, halves[way]])
+
+    first = [buf.at[0, 0, pl.ds(i, 1)] for i in range(RING)]
+    second = [[buf.at[0, d, g] for d in range(RING)] for g in GROUPS]
+
     def spread(gi):
-        g = GROUPS[gi]
-        send(5 + 4 * gi, buf.at[0, 0, g], buf.at[0, 1, g], here.peer(2, 1))
-        send(6 + 4 * gi, buf.at[0, 0, g], buf.at[0, 2, g], here.peer(2, -1))
+        both_ways(1 + gi, second[gi][0], second[gi][1], second[gi][2], 2)
         have(gi, 0)
 
-    def second(gi):
-        g = GROUPS[gi]
-        for d, step in ((1, 1), (2, -1)):
-            arrive(4 + 4 * gi + d, buf.at[0, d, g])
-            lanes = halves[d - 1]
-            send(6 + 4 * gi + d, buf.at[0, d, g, :, :, lanes], buf.at[0, 3, g, :, :, lanes], here.peer(2, step))
-            have(gi, d)
+    def second_relay(gi):
+        relay(1 + gi, second[gi][1], second[gi][2], second[gi][3], 2)
+
+    def second_rest(gi):
+        rest(1 + gi, second[gi][1], second[gi][2])
+        have(gi, 1)
+        have(gi, 2)
 
     def second_far(gi):
-        g = GROUPS[gi]
-        for d in (1, 2):
-            arrive(6 + 4 * gi + d, buf.at[0, 3, g, :, :, halves[d - 1]])
+        far_end(1 + gi, second[gi][3])
         have(gi, 3)
 
     mine = buf.at[0, 0, 0, k]
@@ -410,27 +421,26 @@
     here.barrier()
     for c in loads:
         c.wait()
-    send(0, stage, buf.at[0, 0, 0, k], here.partner)
-    arrive(0, buf.at[0, 0, 0, other])
-    send(1, buf.at[0, 0, 0], buf.at[0, 0, 1], here.peer(1, 1))
-    send(2, buf.at[0, 0, 0], buf.at[0, 0, 2], here.peer(1, -1))
+    send(36, stage, buf.at[0, 0, 0, k], here.partner)
+    arrive(36, buf.at[0, 0, 0, other])
+    both_ways(0, first[0], first[1], first[2], 1)
     spread(0)
-    arrive(1, buf.at[0, 0, 1])
-    send(3, buf.at[0, 0, 1, :, :, halves[0]], buf.at[0, 0, 3, :, :, halves[0]], here.peer(1, 1))
-    arrive(2, buf.at[0, 0, 2])
-    send(4, buf.at[0, 0, 2, :, :, halves[1]], buf.at[0, 0, 3, :, :, halves[1]], here.peer(1, -1))
+    relay(0, first[1], first[2], first[3], 1)
+    second_relay(0)
+    rest(0, first[1], first[2])
     spread(1)
-    second(0)
-    arrive(3, buf.at[0, 0, 3, :, :, halves[0]])
-    arrive(4, buf.at[0, 0, 3, :, :, halves[1]])
+    second_rest(0)
+    far_end(0, first[3])
     spread(2)
-    second(1)
+    second_relay(1)
     second_far(0)
-    second(2)
+    second_rest(1)
+    second_relay(2)
+    second_rest(2)
     second_far(1)
     second_far(2)
     for gi, d in [(gi, d) for d in range(RING) for gi in range(len(GROUPS))]:
-        arrive(17 + 3 * d + gi, buf.at[1, d, GROUPS[gi]])
+        arrive(24 + 3 * d + gi, buf.at[1, d, GROUPS[gi]])
         keep(False, GROUPS[gi], d)
     for c in sent:
         c.wait_send()
@@ -443,7 +453,7 @@
     width = 2 * dm + LANES
     hbm = pl.BlockSpec(memory_space=pltpu.HBM)
     vmem = pl.BlockSpec(memory_space=pltpu.VMEM)
-    sems = pltpu.SemaphoreType.DMA((29,))
+    sems = pltpu.SemaphoreType.DMA((37,))
     return pl.pallas_call(
         gather_kernel,
         out_shape=jax.ShapeDtypeStruct((2, chips, 2, tok_dev, width), BF16),
@@ -583,7 +593,7 @@
             pair_sems, pair_sems, pair_sems, ring_sems, ring_sems,
             pltpu.SemaphoreType.DMA((2,)),
         ],
-        compiler_params=pltpu.CompilerParams(collective_id=1, has_side_effects=True, vmem_limit_bytes=VMEM_LIMIT),
+        compiler_params=pltpu.CompilerParams(collective_id=1, has_side_effects=True, vmem_limit_bytes=60_000_000),
         name="reduce_tokens",
     )(part)
 

time: 120 us -> 104 us (0.87)
  Pallas kernels: 116 us -> 99.2 us
    pallas_call x1, Pallas kernels: 36.2 us -> 26.7 us  [expert_stage(): pl.pallas_call(functools.partial(expert_kernel, dims), out_shape=(jax.Sha...]
    pallas_call x1, Pallas kernels: 49 us -> 43.6 us  [reduce_tokens(): pl.pallas_call(functools.partial(reduce_kernel, dm, top_k), out_shape=(ja...]
    pallas_call x1, Pallas kernels: 30.6 us -> 28.9 us  [gather_tokens(): pl.pallas_call(gather_kernel, out_shape=jax.ShapeDtypeStruct((2, chips, 2...]
where the time goes in v5:
time: 104 us
  Pallas kernels  99.2 us (95%)
  local copies, waits for them, and re-layouts  4.44 us (4%)
    pallas_call x1, Pallas kernels, reduce_tokens(): pl.pallas_call(functools.partial(reduce_kernel, dm, top_k), out_shape=(ja...  43.6 us
    pallas_call x1, Pallas kernels, gather_tokens(): pl.pallas_call(gather_kernel, out_shape=jax.ShapeDtypeStruct((2, chips, 2...  28.9 us
    pallas_call x1, Pallas kernels, expert_stage(): pl.pallas_call(functools.partial(expert_kernel, dims), out_shape=(jax.Sha...  26.7 us
    unnamed x3, local copies, waits for them, and re-layouts  4.44 us

profile of v5, /device:TPU:97, one launch (start us, length us, event | category | flops | bytes accessed | tf_op | source)
XLA Modules:
  0.0 104.3 jit_solution(1506508725642311379)
XLA Ops:
  0.6 28.9 %gather_tokens.1 = bf16[2,16,2,16,2688]{4,3,2,1,0:T(8,128)(2,1)} custom-call(bf16[2,16,1280]{2,1,0:T(8,128)(2,1)} %x_hbm.1, bf16[2,16,1280]{2,1,0:T(8,128)(2,1)} %dy_hbm.1, s32[6,2,16]{2,1,0:T(2,128)} %bitcast.6, f32[6,2,16]{2,1,0:T(2,128)} %bitcast.7), custom_call_target="tpu_custom_call" | custom-call | tf_op jit(solution)/shard_map/gather_tokens/pallas_call | solution.py:457
  29.6 26.7 %experts.1 = (f32[2,512,2688]{2,1,0:T(8,128)}, f32[5,1280,384]{2,1,0:T(8,128)}, f32[5,1280,384]{2,1,0:T(8,128)}, f32[5,384,1280]{2,1,0:T(8,128)}) custom-call(bf16[2,512,2688]{2,1,0:T(8,128)(2,1)} %bitcast.4, bf16[5,1280,384]{2,1,0:T(8,128)(2,1)} %wg_hbm.1, bf16[5,1280,384]{2,1,0:T(8,128)(2,1)} %wu_hbm.1, bf16[5,384,1280]{2,1,0:T(8,128)(2,1)} %wd_hbm.1), custom_call_target="tpu_custom_call" | custom-call | tf_op jit(solution)/shard_map/experts/pallas_call | solution.py:256
  56.3 43.6 %reduce_tokens.1 = (bf16[2,16,1280]{2,1,0:T(8,128)(2,1)}, bf16[2,16,1280]{2,1,0:T(8,128)(2,1)}, f32[2,16,6]{2,1,0:T(8,128)}) custom-call(f32[2,16,2,16,2688]{4,3,2,1,0:T(8,128)} %bitcast.5), custom_call_target="tpu_custom_call" | custom-call | tf_op jit(solution)/shard_map/reduce_tokens/pallas_call | solution.py:578
  99.9 1.4 %copy.13 = f32[2,16,6]{1,0,2:T(2,128)} copy(f32[2,16,6]{2,1,0:T(8,128)} %get-tuple-element.22) | data formatting | bytes 1536
  101.3 1.5 %copy.16 = bf16[2,16,1280]{2,1,0:T(8,128)(2,1)} copy(bf16[2,16,1280]{2,1,0:T(8,128)(2,1)} %get-tuple-element.32) | data formatting | bytes 163840
  102.8 1.5 %copy.17 = bf16[2,16,1280]{2,1,0:T(8,128)(2,1)} copy(bf16[2,16,1280]{2,1,0:T(8,128)(2,1)} %get-tuple-element.33) | data formatting | bytes 163840

commit v6 on v5

--- a/solution.py
+++ b/solution.py
@@ -13,7 +13,8 @@
 BF16 = jnp.bfloat16
 LANES = 128
 SMALL = 32
-VMEM_LIMIT = 66_000_000
+EXPERT_VMEM = 46_000_000
+COMM_VMEM = 30_000_000
 
 
 def dot_nn(a, b):
@@ -40,9 +41,9 @@
     return [(s, min(step, width - s)) for s in range(0, width, step)]
 
 
-def expert_kernel(dims, xd_hbm, wg_hbm, wu_hbm, wd_hbm, part_hbm, gg_hbm, gu_hbm, gd_hbm,
-                  xd_v, pt_v, gr_v, acc_v, wgu_v, wd_v, og_v, ou_v, od_v, pos_v,
-                  xt_v, qt_v, a_v, duv_v, cnt_s, base_s, sem_x, sem_w, sem_o, sem_p):
+def expert_kernel(dims, xd_v, wg_hbm, wu_hbm, wd_hbm, acc_v, gg_hbm, gu_hbm, gd_hbm,
+                  pt_v, gr_v, wgu_v, wd_v, og_v, ou_v, od_v, pos_v,
+                  xt_v, qt_v, a_v, duv_v, cnt_s, base_s, sem_w, sem_o):
     tokens, dm, ff, el, top_k, seg = dims
     n_row, n_col, n_core = lax.axis_size("row"), lax.axis_size("col"), lax.axis_size("core")
     me = (lax.axis_index("row") * n_col + lax.axis_index("col")) * n_core + lax.axis_index("core")
@@ -56,9 +57,9 @@
         return [pltpu.make_async_copy(v.at[slot], h.at[e], sem_o.at[slot, i])
                 for i, (h, v) in enumerate(((gg_hbm, og_v), (gu_hbm, ou_v), (gd_hbm, od_v)))]
 
-    loads_x = [pltpu.make_async_copy(xd_hbm.at[m], xd_v.at[m], sem_x.at[m]) for m in range(2)]
-    for c in loads_x:
-        c.start()
+    for m in range(2):
+        for c in load_w(m, m):
+            c.start()
 
     row_i = lax.broadcasted_iota(jnp.int32, (tokens, tokens), 0)
     col_i = lax.broadcasted_iota(jnp.int32, (tokens, tokens), 1)
@@ -71,9 +72,6 @@
 
     n_chunks = []
     for m in range(2):
-        loads_x[m].wait()
-        for c in load_w(m, m):
-            c.start()
         meta_t = xd_v[m, :, 2 * dm:].astype(F32).T
         hits = jnp.zeros((8, tokens), F32)
         for j in range(top_k):
@@ -237,37 +235,33 @@
             val = raw[:, e:e + 1] + raw[:, 8 + e:9 + e] + raw[:, 16 + e:17 + e]
             out = jnp.where(ids == (me * el + e).astype(F32), val, out)
         acc_v[m, :, 2 * dm:] = out
-        pltpu.make_async_copy(acc_v.at[m], part_hbm.at[m], sem_p.at[m]).start()
 
     for e in range(el - 2, el):
         for c in store_g(e, e % 2):
             c.wait()
-    for m in range(2):
-        pltpu.make_async_copy(acc_v.at[m], part_hbm.at[m], sem_p.at[m]).wait()
 
 
 def expert_stage(xd, w_gate, w_up, w_down, top_k, seg):
     _, tokens, width = xd.shape
     el, dm, ff = w_gate.shape
     any_spec = pl.BlockSpec(memory_space=pltpu.HBM)
+    vmem_spec = pl.BlockSpec(memory_space=pltpu.VMEM)
     rows_max = el * seg
     tile_rows = seg + SMALL
     dims = (tokens, dm, ff, el, top_k, seg)
     return pl.pallas_call(
         functools.partial(expert_kernel, dims),
         out_shape=(
-            jax.ShapeDtypeStruct((2, tokens, width), F32),
-            jax.ShapeDtypeStruct((el, dm, ff), F32),
-            jax.ShapeDtypeStruct((el, dm, ff), F32),
-            jax.ShapeDtypeStruct((el, ff, dm), F32),
+            pltpu.VMEM((2, tokens, width), F32),
+            pltpu.HBM((el, dm, ff), F32),
+            pltpu.HBM((el, dm, ff), F32),
+            pltpu.HBM((el, ff, dm), F32),
         ),
-        in_specs=[any_spec] * 4,
-        out_specs=[any_spec] * 4,
+        in_specs=[vmem_spec] + [any_spec] * 3,
+        out_specs=[vmem_spec] + [any_spec] * 3,
         scratch_shapes=[
-            pltpu.VMEM((2, tokens, width), BF16),
             pltpu.VMEM((2, tokens, rows_max), BF16),
             pltpu.VMEM((2, rows_max, width), BF16),
-            pltpu.VMEM((2, tokens, width), F32),
             pltpu.VMEM((2, dm, 2 * ff), BF16),
             pltpu.VMEM((2, ff, dm), BF16),
             pltpu.VMEM((2, dm, ff), F32),
@@ -280,14 +274,12 @@
             pltpu.VMEM((tile_rows, 2 * ff), BF16),
             pltpu.SMEM((2, 8), jnp.int32),
             pltpu.SMEM((2, 8), jnp.int32),
-            pltpu.SemaphoreType.DMA((2,)),
             pltpu.SemaphoreType.DMA((2, 3)),
             pltpu.SemaphoreType.DMA((2, 3)),
-            pltpu.SemaphoreType.DMA((2,)),
         ],
-        compiler_params=pltpu.CompilerParams(vmem_limit_bytes=VMEM_LIMIT),
+        compiler_params=pltpu.CompilerParams(vmem_limit_bytes=EXPERT_VMEM),
         name="experts",
-    )(xd, w_gate, w_up, w_down)
+    )(pltpu.with_memory_space_constraint(xd, pltpu.VMEM), *(pltpu.with_memory_space_constraint(w, pltpu.HBM) for w in (w_gate, w_up, w_down)))
 
 
 RING = 4
@@ -308,10 +300,6 @@
         row = lax.rem(self.row + (d1 * first + d2 * (1 - first)) + self.n_row, self.n_row)
         col = lax.rem(self.col + (d1 * (1 - first) + d2 * first) + self.n_col, self.n_col)
         return row, col
-
-    def chip(self, first, d1, d2):
-        row, col = self.spot(first, d1, d2)
-        return row * self.n_col + col
 
     def peer(self, axis, d):
         row, col = self.spot(self.core, d, 0) if axis == 1 else self.spot(self.core, 0, d)
@@ -340,7 +328,7 @@
     return dot_tn(rows, eye).astype(BF16)
 
 
-def gather_kernel(x_hbm, dy_hbm, route_ref, gates_ref, out_hbm, buf, stage, send_sem, recv_sem, load_sem, out_sem):
+def gather_kernel(x_hbm, dy_hbm, route_ref, gates_ref, buf, stage, send_sem, recv_sem, load_sem):
     here = Place()
     k, other = here.core, here.other
     dm = x_hbm.shape[2]
@@ -359,16 +347,9 @@
     def arrive(idx, dst):
         move(idx, dst, dst, here.partner).wait_recv()
 
-    def keep(mine, g, d):
-        first = k if mine else other
-        for i in range(g.start, g.stop):
-            c = here.chip(first, NEAR[i], NEAR[d])
-            pltpu.make_async_copy(buf.at[0 if mine else 1, d, i], out_hbm.at[first, c], out_sem.at[0 if mine else 1]).start()
-
     def have(gi, d):
         g = GROUPS[gi]
         send(24 + 3 * d + gi, buf.at[0, d, g], buf.at[1, d, g], here.partner)
-        keep(True, g, d)
 
     def both_ways(p, src, left, right, axis):
         for way, dst in ((0, left), (1, right)):
@@ -441,14 +422,11 @@
     second_far(2)
     for gi, d in [(gi, d) for d in range(RING) for gi in range(len(GROUPS))]:
         arrive(24 + 3 * d + gi, buf.at[1, d, GROUPS[gi]])
-        keep(False, GROUPS[gi], d)
     for c in sent:
         c.wait_send()
-    for n, mb in enumerate((k, other)):
-        pltpu.make_async_copy(out_hbm.at[mb], out_hbm.at[mb], out_sem.at[n]).wait()
-
-
-def gather_tokens(x, grad_y, route_idx, gates, chips):
+
+
+def gather_tokens(x, grad_y, route_idx, gates):
     _, tok_dev, dm = x.shape
     width = 2 * dm + LANES
     hbm = pl.BlockSpec(memory_space=pltpu.HBM)
@@ -456,29 +434,28 @@
     sems = pltpu.SemaphoreType.DMA((37,))
     return pl.pallas_call(
         gather_kernel,
-        out_shape=jax.ShapeDtypeStruct((2, chips, 2, tok_dev, width), BF16),
+        out_shape=pltpu.VMEM((2, RING, RING, 2, tok_dev, width), BF16),
         in_specs=[hbm, hbm, vmem, vmem],
-        out_specs=hbm,
-        scratch_shapes=[pltpu.VMEM((2, RING, RING, 2, tok_dev, width), BF16), pltpu.VMEM((tok_dev, width), BF16),
-                        sems, sems, pltpu.SemaphoreType.DMA((4,)), pltpu.SemaphoreType.DMA((2,))],
-        compiler_params=pltpu.CompilerParams(collective_id=0, has_side_effects=True, vmem_limit_bytes=VMEM_LIMIT),
+        out_specs=vmem,
+        scratch_shapes=[pltpu.VMEM((tok_dev, width), BF16), sems, sems, pltpu.SemaphoreType.DMA((4,))],
+        compiler_params=pltpu.CompilerParams(collective_id=0, has_side_effects=True, vmem_limit_bytes=COMM_VMEM),
         name="gather_tokens",
-    )(x, grad_y, jnp.transpose(route_idx, (2, 0, 1)), jnp.transpose(gates, (2, 0, 1)))
-
-
-def reduce_kernel(dm, top_k, part_hbm, y_ref, dx_ref, dg_ref, own, pair, full, half, last, load_sem, pair_send, pair_recv,
+    )(pltpu.with_memory_space_constraint(x, pltpu.HBM), pltpu.with_memory_space_constraint(grad_y, pltpu.HBM), jnp.transpose(route_idx, (2, 0, 1)), jnp.transpose(gates, (2, 0, 1)))
+
+
+def reduce_kernel(dm, top_k, part_ref, y_ref, dx_ref, dg_ref, own, pair, full, half, last, pair_send, pair_recv,
                   ring_send, ring_recv, last_sem):
     here = Place()
     k, other = here.core, here.other
-    halves = half_lanes(part_hbm.shape[4])
+    halves = half_lanes(part_ref.shape[5])
     sent = []
 
-    def load(d, i):
-        return pltpu.make_async_copy(part_hbm.at[k, here.chip(k, FAR[i], FAR[d])], own.at[d, i], load_sem.at[d, i])
+    def near_at(n):
+        return NEAR.index(FAR[n])
 
     def swap(d, i):
-        return pltpu.make_async_remote_copy(src_ref=part_hbm.at[other, here.chip(other, FAR[i], FAR[d])], dst_ref=pair.at[d, i],
-                                            send_sem=pair_send.at[d, i], recv_sem=pair_recv.at[d, i], device_id=here.partner, device_id_type=MESH)
+        return pltpu.make_async_remote_copy(src_ref=part_ref.at[1, near_at(d), near_at(i)], dst_ref=pair.at[d, i], send_sem=pair_send.at[d, i],
+                                            recv_sem=pair_recv.at[d, i], device_id=here.partner, device_id_type=MESH)
 
     def move(f, kind, src, dst, axis):
         return pltpu.make_async_remote_copy(src_ref=src, dst_ref=dst, send_sem=ring_send.at[f, kind], recv_sem=ring_recv.at[f, kind],
@@ -494,9 +471,8 @@
 
     def add_pair(d, gi):
         for i in range(GROUPS[gi].start, GROUPS[gi].stop):
-            load(d, i).wait()
             swap(d, i).wait_recv()
-            own[d, i] = own[d, i] + pair[d, i]
+            own[d, i] = part_ref[0, near_at(d), near_at(i)] + pair[d, i]
 
     def far(f, src, g, axis):
         for kind in range(2):
@@ -531,8 +507,6 @@
         done(gi, GROUPS[gi], GROUPS[gi])
 
     order = [(0, 0), (0, 1), (0, 2), (2, 0), (1, 0), (0, 3), (2, 1), (2, 2), (1, 1), (1, 2), (3, 0), (2, 3), (1, 3), (3, 1), (3, 2), (3, 3)]
-    for q in order:
-        load(*q).start()
     here.barrier()
     for q in order:
         c = swap(*q)
@@ -570,7 +544,7 @@
 
 
 def reduce_tokens(part, dm, top_k):
-    _, chips, cores, tok_dev, width = part.shape
+    _, _, _, cores, tok_dev, width = part.shape
     vmem = pl.BlockSpec(memory_space=pltpu.VMEM)
     block = (cores, tok_dev, width)
     ring_sems = pltpu.SemaphoreType.DMA((4, 4))
@@ -582,7 +556,7 @@
             jax.ShapeDtypeStruct((2, tok_dev, dm), BF16),
             jax.ShapeDtypeStruct((2, tok_dev, top_k), F32),
         ),
-        in_specs=[pl.BlockSpec(memory_space=pltpu.HBM)],
+        in_specs=[vmem],
         out_specs=(vmem, vmem, vmem),
         scratch_shapes=[
             pltpu.VMEM((RING, RING) + block, F32),
@@ -590,12 +564,12 @@
             pltpu.VMEM((2, RING + 1) + block, F32),
             pltpu.VMEM((RING + 1,) + block, F32),
             pltpu.VMEM((tok_dev, width), F32),
-            pair_sems, pair_sems, pair_sems, ring_sems, ring_sems,
+            pair_sems, pair_sems, ring_sems, ring_sems,
             pltpu.SemaphoreType.DMA((2,)),
         ],
-        compiler_params=pltpu.CompilerParams(collective_id=1, has_side_effects=True, vmem_limit_bytes=60_000_000),
+        compiler_params=pltpu.CompilerParams(collective_id=1, has_side_effects=True, vmem_limit_bytes=COMM_VMEM),
         name="reduce_tokens",
-    )(part)
+    )(pltpu.with_memory_space_constraint(part, pltpu.VMEM))
 
 
 def solution(mesh):
@@ -607,10 +581,9 @@
         _, tok_dev, dm = x.shape
         top_k = route_idx.shape[2]
         width = 2 * dm + LANES
-        chips = group // 2
-        xd = gather_tokens(x, grad_y, route_idx, gates, chips).reshape(2, group * tok_dev, width)
+        xd = gather_tokens(x, grad_y, route_idx, gates).reshape(2, group * tok_dev, width)
         part, g_gate, g_up, g_down = expert_stage(xd, w_gate, w_up, w_down, top_k, group * (tok_dev // 2))
-        y, dx, dg = reduce_tokens(part.reshape(2, chips, 2, tok_dev, width), dm, top_k)
+        y, dx, dg = reduce_tokens(part.reshape(2, RING, RING, 2, tok_dev, width), dm, top_k)
         return y, dx, dg, g_gate, g_up, g_down
 
     return jax.shard_map(moe_layer, mesh=mesh, in_specs=(tok_spec, tok_spec, tok_spec, w_spec, w_spec, w_spec, tok_spec), out_specs=(tok_spec, tok_spec, tok_spec, w_spec, w_spec, w_spec), check_vma=False)

time: 104 us -> 97.4 us (0.937)
  Pallas kernels: 99.2 us -> 93.6 us
  local copies, waits for them, and re-layouts: 4.44 us -> 3.32 us
    pallas_call x2, Pallas kernels: 55.6 us -> 49.9 us  [the longest x1 27.6 us: gather_tokens(): pl.pallas_call(gather_kernel, out_shape=pltpu.VMEM((2, RING, RING, 2, tok...]
    unnamed x3 -> x7, local copies, waits for them, and re-layouts: 4.44 us -> 3.32 us
where the time goes in v6:
time: 97.4 us; the launch traced here: 97.6 us
  Pallas kernels  93.6 us (96%)
  local copies, waits for them, and re-layouts  3.32 us (3%)
    pallas_call x1, Pallas kernels, reduce_tokens(): pl.pallas_call(functools.partial(reduce_kernel, dm, top_k), out_shape=(ja...  43.7 us
    pallas_call x1, Pallas kernels, gather_tokens(): pl.pallas_call(gather_kernel, out_shape=pltpu.VMEM((2, RING, RING, 2, tok...  27.6 us
    pallas_call x1, Pallas kernels, expert_stage(): pl.pallas_call(functools.partial(expert_kernel, dims), out_shape=(pltpu.V...  22.3 us
    unnamed x7, local copies, waits for them, and re-layouts  3.32 us

profile of v6, /device:TPU:97, one launch (start us, length us, event | category | flops | bytes accessed | tf_op | source)
XLA Modules:
  0.0 97.6 jit_solution(15798274832913719426)
XLA Ops:
  0.6 0.0 copy-start
  0.6 0.7 copy-done
  1.3 0.0 copy-start.1
  1.3 0.7 copy-done.1
  2.0 27.6 %gather_tokens.1 = bf16[2,4,4,2,16,2688]{5,4,3,2,1,0:T(8,128)(2,1)S(1)} custom-call(bf16[2,16,1280]{2,1,0:T(8,128)(2,1)} %x_hbm.1, bf16[2,16,1280]{2,1,0:T(8,128)(2,1)} %dy_hbm.1, s32[6,2,16]{2,1,0:T(2,128)S(1)} %bitcast.6, f32[6,2,16]{2,1,0:T(2,128)S(1)} %bitcast.7), custom_call_target="tpu_custom_call" | custom-call | tf_op jit(solution)/shard_map/gather_tokens/pallas_call | solution.py:435
  29.6 22.3 %experts.1 = (f32[2,512,2688]{2,1,0:T(8,128)S(1)}, f32[5,1280,384]{2,1,0:T(8,128)}, f32[5,1280,384]{2,1,0:T(8,128)}, f32[5,384,1280]{2,1,0:T(8,128)}) custom-call(bf16[2,512,2688]{2,1,0:T(8,128)(2,1)S(1)} %bitcast.4, bf16[5,1280,384]{2,1,0:T(8,128)(2,1)} %wg_hbm.1, bf16[5,1280,384]{2,1,0:T(8,128)(2,1)} %wu_hbm.1, bf16[5,384,1280]{2,1,0:T(8,128)(2,1)} %wd_hbm.1), custom_call_target="tpu_custom_call" | custom-call | tf_op jit(solution)/shard_map/experts/pallas_call | solution.py:252
  51.9 43.7 %reduce_tokens.1 = (bf16[2,16,1280]{2,1,0:T(8,128)(2,1)S(1)}, bf16[2,16,1280]{2,1,0:T(8,128)(2,1)S(1)}, f32[2,16,6]{2,1,0:T(8,128)S(1)}) custom-call(f32[2,4,4,2,16,2688]{5,4,3,2,1,0:T(8,128)S(1)} %bitcast.5), custom_call_target="tpu_custom_call" | custom-call | tf_op jit(solution)/shard_map/reduce_tokens/pallas_call | solution.py:552
  95.6 0.7 copy.13
  96.3 0.6 copy.16
  96.9 0.6 copy.17
Async XLA Ops:
  0.6 0.7 copy-start
  1.3 0.7 copy-start.1
